TPU v7x, 256 devices: a whole 4x4x8 slice. The times are simulated.
256 devices in a mesh: row: 16 (over x, y), col: 16 (over z, core).
Axes of the slice: x: 4, y: 4, z: 8, core: 2. Of those that a mesh axis runs over, the one named last changes fastest.
Arguments:
- points: bfloat16 [40960, 64], P(('row', 'col')), may hold values from -5 to 5
- start_vectors: bfloat16 [40960, 32], P(('row', 'col')), may hold values from -12 to 12
Outputs:
- basis: float32 [40960, 32], P(('row', 'col'))
All inputs are finite; a program needn't handle non-finite values.
Results may differ from a plain program's by a relative error of at most 0.007.
Values may be sent and summed in bfloat16 or wider, within the bound.
A program may use at most 64 MiB of HBM per device.

v0:
```python
import functools

import jax
import jax.numpy as jnp
from jax import lax
from jax.sharding import Mesh
from jax.sharding import PartitionSpec as P

ITERS = 2
ROW = ("row_0", "row_1")
ROW_COL = ("row_0", "row_1", "col")


KERNEL_SCALE = 5.12


def one_axis_at_a_time(shard, axes):
    return functools.reduce(lax.psum, axes, shard)


def in_order(pieces, dim):
    dims = list(pieces.shape[1:])
    dims[dim] *= pieces.shape[0]
    return jnp.moveaxis(pieces, 0, dim).reshape(dims)


def sent_to_all(shard, axis):
    size = lax.axis_size(axis)
    return lax.all_to_all(
        jnp.broadcast_to(shard[None], (size, *shard.shape)), axis, 0, 0, tiled=True
    )


def gather_directly(shard, axis, dim):
    return in_order(sent_to_all(shard, axis), dim)


def gathered_total(shard, axis):
    pieces = lax.all_gather(shard, axis)
    return pieces.sum(axis=0)


def squared_norms(values):
    return jnp.sum(jnp.square(values.astype(jnp.float32)), axis=1)


def affinity(block_pts, block_sq, col_pts, col_sq):
    features = block_pts.shape[1]
    cross = lax.dot_general(
        block_pts, col_pts, (((1,), (1,)), ((), ())), preferred_element_type=jnp.float32
    )
    dist = block_sq[:, None] + col_sq[None, :] - 2.0 * cross
    return jnp.exp(dist * (-KERNEL_SCALE / features)).astype(jnp.bfloat16)


def sweep(row_pts, row_sq, col_pts, col_sq, panel, with_degree):
    rows, features = row_pts.shape
    height = min(512, rows)
    count = rows // height
    stacked = (row_pts.reshape(count, height, features), row_sq.reshape(count, height))

    def one_block(item):
        weights = affinity(item[0], item[1], col_pts, col_sq)
        results = ()
        if panel is not None:
            results = results + (jnp.dot(weights, panel, preferred_element_type=jnp.float32),)
        if with_degree:
            results = results + (jnp.sum(weights, axis=1, dtype=jnp.float32),)
        return results

    mapped = lax.map(one_block, stacked)
    return [piece.reshape((rows,) + piece.shape[2:]) for piece in mapped]


def orthonormal(product, degree, total, group, offset):
    scaled = product / degree[:, None]
    gram_part = jnp.dot(scaled.T, scaled, preferred_element_type=jnp.float32)
    gram = one_axis_at_a_time(gram_part, ROW)
    mine = lax.dynamic_slice_in_dim(scaled, offset, group, 0)
    lower = jnp.linalg.cholesky(gram / total)
    return lax.linalg.triangular_solve(lower, mine, left_side=False, lower=True, transpose_a=True)


def shards(points, start_vectors):
    group = points.shape[0]
    total = group * lax.axis_size(ROW) * lax.axis_size("col")
    offset = lax.axis_index("col") * group
    row_pts = gather_directly(points, "col", 0)
    col_pts = gather_directly(points, ROW, 0)
    row_sq = squared_norms(row_pts)
    col_sq = squared_norms(col_pts)
    degree_part = sweep(row_pts, row_sq, col_pts, col_sq, None, True)[0]
    vectors = start_vectors
    ortho = jnp.zeros(start_vectors.shape, jnp.float32)
    degree = None
    for step in range(ITERS):
        panel = gather_directly(vectors, ROW, 0)
        if step == 0:
            product_part = sweep(row_pts, row_sq, col_pts, col_sq, panel, False)[0]
            product, degree = (
                gathered_total(product_part, "col"),
                gathered_total(degree_part, "col"),
            )
        else:
            product_part = sweep(row_pts, row_sq, col_pts, col_sq, panel, False)[0]
            product = gathered_total(product_part, "col")
        ortho = orthonormal(product, degree, total, group, offset)
        vectors = ortho.astype(jnp.bfloat16)
    return ortho


def solution(mesh):
    finer = Mesh(mesh.devices.reshape(4, 4, mesh.shape["col"]), ("row_0", "row_1", "col"))
    in_specs = (P(ROW_COL, None), P(ROW_COL, None))
    out_specs = P(ROW_COL, None)
    return jax.shard_map(
        shards, mesh=finer, in_specs=in_specs, out_specs=out_specs, check_vma=False
    )
```

profile of v0, /device:TPU:32, one launch (start us, length us, event | category | flops | bytes accessed | tf_op | source)
XLA Modules:
  0.0 276.3 jit_solution(24421918623637520)
XLA Ops:
  7.3 15.3 %all_to_all.20 = bf16[16,160,32]{1,2,0:T(8,128)(2,1)S(1)} all-to-all(bf16[16,160,32]{1,2,0:T(8,128)(2,1)S(1)} %broadcast_in_dim.21), channel_id=1, replica_groups=mesh['row_0'=4,'row_1'=4,'col'=16] {'row_0','row_1'}, dimensions={0} | all-to-all | bytes 327680 | tf_op jit(solution)/shard_map/all_to_all | solution.py:29
  24.2 14.0 %all_to_all.21 = bf16[16,160,64]{1,2,0:T(8,128)(2,1)S(1)} all-to-all(bf16[16,160,64]{1,2,0:T(8,128)(2,1)} %broadcast_in_dim.20), channel_id=1, replica_groups=mesh['row_0'=4,'row_1'=4,'col'=16] {'row_0','row_1'}, dimensions={0} | all-to-all | bytes 655360 | tf_op jit(solution)/shard_map/all_to_all | solution.py:29
  38.2 8.6 %all-to-all-start = ((bf16[16,160,64]{1,2,0:T(8,128)(2,1)}), bf16[16,160,64]{1,2,0:T(8,128)(2,1)S(1)}, u32[]{:S(2)}, u32[]{:S(2)}) async-start(bf16[16,160,64]{1,2,0:T(8,128)(2,1)} %broadcast_in_dim.20), calls=%async_computation | async-start | bytes 1048576 | tf_op jit(solution)/shard_map/all_to_all | solution.py:29
  47.7 13.3 %all-to-all-done = bf16[16,160,64]{1,2,0:T(8,128)(2,1)S(1)} async-done(((bf16[16,160,64]{1,2,0:T(8,128)(2,1)}), bf16[16,160,64]{1,2,0:T(8,128)(2,1)S(1)}, u32[]{:S(2)}, u32[]{:S(2)}) %all-to-all-start) | async-done | bytes 327712 | tf_op jit(solution)/shard_map/all_to_all | solution.py:29
  61.7 13.0 %while.30 = (s32[]{:T(128)}, f32[5,512,32]{1,0,2:T(8,128)S(1)}, f32[5,512]{1,0:T(8,128)S(1)}, f32[2560]{0:T(1024)S(1)}, bf16[5,512,64]{2,1,0:T(8,128)(2,1)S(1)},...) while((s32[]{:T(128)}, f32[5,512,32]{1,0,2:T(8,128)S(1)}, ...), condition=%wide.region_3.4_spmd, body=%wide.region_2.3_spmd.sunk | while | flops 258211840 | bytes 1788009 | solution.py:71
  69.5 1.9 fusion.60
  75.6 8.0 %while.31 = (s32[]{:T(128)}, f32[5,512]{1,0:T(8,128)S(1)}, f32[5,512]{1,0:T(8,128)S(1)}, f32[2560]{0:T(1024)S(1)}, bf16[5,512,64]{2,1,0:T(8,128)(2,1)S(1)}, /*in...) while((s32[]{:T(128)}, f32[5,512]{1,0:T(8,128)S(1)}, f32[5,512]{1,0:T(8,128)S(1)}, f32[2560]{0:T(1024)S(1)}, ...), condition=%wide.region_7.8_spmd, body=%wide.region_5.7_spmd.sunk | while | flops 176946688 | bytes 811105 | solution.py:71
  83.7 16.9 %all-gather = f32[16,1,2560]{2,1,0:T(1,128)S(1)} all-gather(f32[1,1,2560]{2,1,0:T(1,128)S(1)} %reshape.48), channel_id=1, replica_groups=mesh['row_0'=4,'row_1'=4,'col'=16] {'col'}, dimensions={0}, use_global_device_ids=true | all-gather | bytes 174080 | tf_op jit(solution)/shard_map/all_gather | solution.py:39
  100.7 14.7 %all-gather.4.cloned.1.call-done = f32[16,2560,32]{1,2,0:T(8,128)} async-done(((f32[1,2560,32]{1,2,0:T(8,128)}), f32[16,2560,32]{1,2,0:T(8,128)}) %all-gather.4.cloned.1.call-update) | async-done | bytes 5242896 | tf_op jit(solution)/shard_map/all_gather | solution.py:39
  115.4 2.8 %reduce_sum.59 = f32[2560,32]{0,1:T(8,128)S(1)} reduce(f32[16,2560,32]{1,2,0:T(8,128)} %all-gather.4.cloned.1.call-done, f32[]{:T(128)} %constant.84.clone.1), dimensions={0}, to_apply=%region_4.5 | reduce | flops 1228800 | bytes 5570564 | tf_op jit(solution)/shard_map/reduce_sum | solution.py:40
  118.4 17.0 %psum.28 = f32[32,32]{0,1:T(8,128)S(1)} all-reduce(f32[32,32]{0,1:T(8,128)S(1)} %fusion.36), channel_id=1, replica_groups=mesh['row_0'=4,'row_1'=4,'col'=16] {'row_0'}, use_global_device_ids=true, to_apply=%region_9.10 | all-reduce | flops 1024 | bytes 8192 | tf_op jit(solution)/shard_map/psum | solution.py:18
  135.4 16.7 %psum.29 = f32[32,32]{0,1:T(8,128)S(1)} all-reduce(f32[32,32]{0,1:T(8,128)S(1)} %psum.28), channel_id=1, replica_groups=mesh['row_0'=4,'row_1'=4,'col'=16] {'row_1'}, use_global_device_ids=true, to_apply=%region_10.11 | all-reduce | flops 1024 | bytes 8192 | tf_op jit(solution)/shard_map/psum | solution.py:18
  152.2 2.9 %cholesky.44 = f32[32,32]{1,0:T(8,128)S(1)} custom-call(f32[32,32]{1,0:T(8,128)S(1)} %fusion.31), custom_call_target="Cholesky" | custom-call | tf_op jit(solution)/shard_map/jit(cholesky)/cholesky | solution.py:80
  156.5 2.4 custom-call.6
  159.9 3.5 %all-to-all-start.3 = ((bf16[16,160,32]{1,2,0:T(8,128)(2,1)}), bf16[16,160,32]{1,2,0:T(8,128)(2,1)S(1)}, u32[]{:S(2)}, u32[]{:S(2)}) async-start(bf16[16,160,32]{1,2,0:T(8,128)(2,1)} %broadcast_in_dim.26), calls=%async_computation.3 | async-start | bytes 524288 | tf_op jit(solution)/shard_map/all_to_all | solution.py:29
  163.5 8.4 %all-to-all-done.3 = bf16[16,160,32]{1,2,0:T(8,128)(2,1)S(1)} async-done(((bf16[16,160,32]{1,2,0:T(8,128)(2,1)}), bf16[16,160,32]{1,2,0:T(8,128)(2,1)S(1)}, u32[]{:S(2)}, u32[]{:S(2)}) %all-to-all-start.3) | async-done | bytes 163872 | tf_op jit(solution)/shard_map/all_to_all | solution.py:29
  172.3 13.0 %while.32 = (s32[]{:T(128)}, f32[5,512,32]{1,0,2:T(8,128)S(1)}, f32[5,512]{1,0:T(8,128)S(1)}, f32[2560]{0:T(1024)S(1)}, bf16[5,512,64]{2,1,0:T(8,128)(2,1)S(1)},...) while((s32[]{:T(128)}, f32[5,512,32]{1,0,2:T(8,128)S(1)}, ...), condition=%wide.region_14.17_spmd, body=%wide.region_13.16_spmd.sunk | while | flops 258211840 | bytes 1788009 | solution.py:71
  180.1 1.9 fusion.66
  186.2 38.9 %all-gather.6.cloned.1.call-done = f32[16,2560,32]{1,2,0:T(8,128)} async-done(((f32[1,2560,32]{1,2,0:T(8,128)}), f32[16,2560,32]{1,2,0:T(8,128)}) %all-gather.6.cloned.1.call-update) | async-done | bytes 5242896 | tf_op jit(solution)/shard_map/all_gather | solution.py:39
  225.1 2.8 %reduce_sum.61 = f32[2560,32]{0,1:T(8,128)S(1)} reduce(f32[16,2560,32]{1,2,0:T(8,128)} %all-gather.6.cloned.1.call-done, f32[]{:T(128)} %constant.84.clone.1), dimensions={0}, to_apply=%region_15.18 | reduce | flops 1228800 | bytes 5570564 | tf_op jit(solution)/shard_map/reduce_sum | solution.py:40
  228.0 16.8 %psum.30 = f32[32,32]{0,1:T(8,128)S(1)} all-reduce(f32[32,32]{0,1:T(8,128)S(1)} %fusion.37), channel_id=1, replica_groups=mesh['row_0'=4,'row_1'=4,'col'=16] {'row_0'}, use_global_device_ids=true, to_apply=%region_16.19 | all-reduce | flops 1024 | bytes 8192 | tf_op jit(solution)/shard_map/psum | solution.py:18
  244.9 16.9 %psum.31 = f32[32,32]{0,1:T(8,128)S(1)} all-reduce(f32[32,32]{0,1:T(8,128)S(1)} %psum.30), channel_id=1, replica_groups=mesh['row_0'=4,'row_1'=4,'col'=16] {'row_1'}, use_global_device_ids=true, to_apply=%region_17.20 | all-reduce | flops 1024 | bytes 8192 | tf_op jit(solution)/shard_map/psum | solution.py:18
  261.9 2.9 %cholesky.55 = f32[32,32]{1,0:T(8,128)S(1)} custom-call(f32[32,32]{1,0:T(8,128)S(1)} %fusion.29), custom_call_target="Cholesky" | custom-call | tf_op jit(solution)/shard_map/jit(cholesky)/cholesky | solution.py:80
  266.1 2.4 custom-call.7
  (93 shorter events, 41.1 us)
Async XLA Ops:
  38.2 22.8 %all-to-all-start = ((bf16[16,160,64]{1,2,0:T(8,128)(2,1)}), bf16[16,160,64]{1,2,0:T(8,128)(2,1)S(1)}, u32[]{:S(2)}, u32[]{:S(2)}) async-start(bf16[16,160,64]{1,2,0:T(8,128)(2,1)} %broadcast_in_dim.20), calls=%async_computation | async-start | bytes 1048576 | tf_op jit(solution)/shard_map/all_to_all | solution.py:29
  46.8 68.7 %all-gather.4.cloned.1.call-start = ((), (), s32[]{:S(2)}) async-start(), calls=%async_computation.4 | async-start | bytes 5570560 | tf_op jit(solution)/shard_map/all_gather | solution.py:39
  159.9 12.0 %all-to-all-start.3 = ((bf16[16,160,32]{1,2,0:T(8,128)(2,1)}), bf16[16,160,32]{1,2,0:T(8,128)(2,1)S(1)}, u32[]{:S(2)}, u32[]{:S(2)}) async-start(bf16[16,160,32]{1,2,0:T(8,128)(2,1)} %broadcast_in_dim.26), calls=%async_computation.3 | async-start | bytes 524288 | tf_op jit(solution)/shard_map/all_to_all | solution.py:29
  163.4 61.6 %all-gather.6.cloned.1.call-start = ((), (), s32[]{:S(2)}) async-start(), calls=%async_computation.5 | async-start | bytes 5570560 | tf_op jit(solution)/shard_map/all_gather | solution.py:39
Sparse Core Ops, SparseCore 0:
  75.8 39.6 all-gather.3
  186.3 38.7 all-gather.5
where the time goes:
time: 277 us; the launch traced here: 276 us
  blocking collectives  114 us (41%)
  waiting for transfers between devices  75.3 us (27%)
  matrix products  27.8 us (10%)
  other arithmetic  19.4 us (7%)
  local copies, waits for them, and re-layouts  13.8 us (5%)
  between operations  13.6 us (5%)
  starting transfers between devices  12.2 us (4%)
    psum x4, blocking collectives, one_axis_at_a_time(): return functools.reduce(lax.psum, axes, shard)  67.4 us
    all_gather x2, waiting for transfers between devices, gathered_total(): pieces = lax.all_gather(shard, axis)  53.6 us
    all_to_all x2, blocking collectives, sent_to_all(): lax.all_to_all(jnp.broadcast_to(shard[None], (size, *shard.shape)), axis,...  29.3 us
    all_to_all x2, waiting for transfers between devices, sent_to_all(): lax.all_to_all(jnp.broadcast_to(shard[None], (size, *shard.shape)), axis,...  21.7 us
    dot_general x10, matrix products, one_block(): jnp.dot(weights, panel, preferred_element_type=jnp.float32)  18.8 us
    all_gather x1, blocking collectives, gathered_total(): pieces = lax.all_gather(shard, axis)  16.9 us
    all_to_all x2, starting transfers between devices, sent_to_all(): lax.all_to_all(jnp.broadcast_to(shard[None], (size, *shard.shape)), axis,...  12.1 us
    dot_general x5, matrix products, affinity(): lax.dot_general(block_pts, col_pts, (((1,), (1,)), ((), ())), preferred_e...  7.56 us
  transfers between devices with their start and end apart: 4, of which 4 were waited for; matrix products, arithmetic and copies ran while one was open for 3% of the time, Pallas kernels for 0%

commit v1 on v0

v1 whole, which is shorter than its diff:
```python
import functools
import math

import jax
import jax.numpy as jnp
from jax import lax
from jax.experimental import pallas as pl
from jax.experimental.pallas import tpu as pltpu
from jax.sharding import PartitionSpec as P

MESH = pl.DeviceIdType.MESH
F32 = jnp.float32
BF16 = jnp.bfloat16
HIGHEST = lax.Precision.HIGHEST

KERNEL_SCALE = 5.12
F = 64
K = 32
OWN = 160
LANES = 128
TAIL = OWN - LANES
GROUP = 4 * OWN
NZ = 8
NX = 4
NY = 4
NXY = NX * NY
NCOL = 2 * NZ
ROWS_I = NZ * OWN
COLS_J = 2 * NXY * OWN
TOTAL = 256 * OWN


def lane_block():
    return lax.broadcasted_iota(jnp.int32, (8, LANES), 1) // TAIL


def roll_lanes(x, shift):
    shift = shift % LANES
    return x if shift == 0 else pltpu.roll(x, shift, 1)


def pick(blocks, pieces):
    out = pieces[3]
    for b in (2, 1, 0):
        out = jnp.where(blocks == b, pieces[b], out)
    return out


def transposed_blocks(tiles):
    rows = tiles[0].shape[0]
    blocks = lax.broadcasted_iota(jnp.int32, (rows, LANES), 1) // TAIL
    return [
        pick(blocks, [roll_lanes(tiles[b], TAIL * (b - g)) for b in range(4)]) for g in range(4)
    ]


def packed_tail(tail, rows):
    groups = tail.shape[0] // rows
    return sum(roll_lanes(tail[g * rows : (g + 1) * rows], TAIL * g) for g in range(groups))


def unpacked_tail(packed, groups):
    rows = packed.shape[0]
    keep = lax.broadcasted_iota(jnp.int32, (rows, LANES), 1) < TAIL
    return jnp.concatenate(
        [jnp.where(keep, roll_lanes(packed, -TAIL * g), 0.0) for g in range(groups)], axis=0
    )


def bf16_pieces(x):
    hi = x.astype(BF16).astype(F32)
    rest = x - hi
    mid = rest.astype(BF16).astype(F32)
    return hi, mid, rest - mid


def extended(x, for_rows):
    hi, mid, lo = bf16_pieces(jnp.sum(x * x, axis=0, keepdims=True))
    r = lax.broadcasted_iota(jnp.int32, (8, LANES), 0)
    if for_rows:
        x = 2.0 * x
        head = jnp.where(r == 3, -hi, jnp.where(r == 4, -mid, jnp.where(r == 5, -lo, 0.0)))
        extra = jnp.where(r < 3, -1.0, head)
    else:
        head = jnp.where(r == 0, hi, jnp.where(r == 1, mid, jnp.where(r == 2, lo, 0.0)))
        extra = jnp.where((r >= 3) & (r < 6), 1.0, head)
    return jnp.concatenate([x, extra, jnp.zeros((LANES - F - 8, LANES), F32)], axis=0)


def eliminate(gram, right):
    cols = [jnp.broadcast_to(gram[:, m : m + 1], (K, LANES)) for m in range(K)]
    width = right.shape[1] // LANES
    sub = lax.broadcasted_iota(jnp.int32, (8, LANES), 0)
    cols = [[c[8 * g : 8 * g + 8] for g in range(4)] for c in cols]
    rt = [
        [right[8 * g : 8 * g + 8, w * LANES : (w + 1) * LANES] for w in range(width)]
        for g in range(4)
    ]
    out_rows = []
    for k in range(K):
        kg, kr = k // 8, k % 8
        pivot = cols[k][kg][kr : kr + 1]
        inv = 1.0 / pivot
        factor = [None] * 4
        for g in range(kg, 4):
            f = cols[k][g] * inv
            if g == kg:
                f = jnp.where(sub > kr, f, 0.0)
            factor[g] = f
        for m in range(k + 1, K):
            mg, mr = m // 8, m % 8
            upper = cols[k][mg][mr : mr + 1]
            for g in range(mg, 4):
                cols[m][g] = cols[m][g] - factor[g] * upper
        rows = [rt[kg][w][kr : kr + 1] for w in range(width)]
        scale = lax.rsqrt(pivot)
        out_rows.append([row * scale for row in rows])
        for g in range(kg, 4):
            for w in range(width):
                rt[g][w] = rt[g][w] - factor[g] * rows[w]
    tiles = []
    for g in range(4):
        tile = []
        for w in range(width):
            acc = jnp.broadcast_to(out_rows[8 * g][w], (8, LANES))
            for r in range(1, 8):
                acc = jnp.where(sub == r, out_rows[8 * g + r][w], acc)
            tile.append(acc)
        tiles.append(jnp.concatenate(tile, axis=1) if width > 1 else tile[0])
    return jnp.concatenate(tiles, axis=0)


def kernel(
    pts_ref, vec_ref, out_ref,
    stage, zbuf, jbuf, xi, xj, panel, aff, acc, psend, precv, sbuf, gsend, grecv,
    z_s, z_r, xy_s, xy_r, f_s, f_r, p_s, p_r, s_s, s_r, sf_s, sf_r, ga_s, ga_r, gb_s, gb_r,
):
    row = lax.axis_index("row")
    col = lax.axis_index("col")
    x, y = row // NY, lax.rem(row, NY)
    z, core = col // 2, lax.rem(col, 2)

    def xy_peer(e):
        to_x = lax.rem(x + e // NY, NX)
        to_y = lax.rem(y + e % NY, NY)
        return (to_x * NY + to_y, col)

    def z_peer(d):
        return (row, lax.rem(z + d + NZ, NZ) * 2 + core)

    def col_peer(d):
        return (row, lax.rem(col + d, NCOL))

    partner = (row, z * 2 + 1 - core)

    def remote(src, dst, send, recv, to):
        return pltpu.make_async_remote_copy(
            src_ref=src, dst_ref=dst, send_sem=send, recv_sem=recv,
            device_id=to, device_id_type=MESH,
        )

    barrier = pltpu.get_barrier_semaphore()
    for d in range(1, NCOL):
        pl.semaphore_signal(barrier, inc=1, device_id=col_peer(d), device_id_type=MESH)
    for e in range(1, NXY):
        pl.semaphore_signal(barrier, inc=1, device_id=xy_peer(e), device_id_type=MESH)

    stage[...] = jnp.zeros_like(stage)
    stage[0:OWN, 0:F] = pts_ref[...].astype(F32)
    stage[0:OWN, F : F + K] = vec_ref[...].astype(F32)
    t = stage[...].T
    jbuf[0, 0, 0:64, :] = t[0:F, 0:LANES].astype(BF16)
    jbuf[0, 0, 64:80, :] = packed_tail(t[0:F, LANES:], 16).astype(BF16)
    jbuf[0, 0, 80:112, :] = t[F : F + K, 0:LANES].astype(BF16)
    jbuf[0, 0, 112:128, :] = packed_tail(t[F : F + K, LANES:], 16).astype(BF16)

    pl.semaphore_wait(barrier, NCOL - 1 + NXY - 1)

    def z_copy(d):
        return remote(jbuf.at[0, 0, pl.ds(0, 80)], zbuf.at[d], z_s.at[d], z_r.at[d], z_peer(d))

    def xy_copy(e):
        return remote(jbuf.at[0, 0], jbuf.at[0, e], xy_s.at[e], xy_r.at[e], xy_peer(e))

    def forward(e):
        return remote(jbuf.at[0, e], jbuf.at[1, e], f_s.at[e], f_r.at[e], partner)

    for d in range(1, NZ):
        z_copy(d).start()
    for e in range(1, NXY):
        xy_copy(e).start()
    forward(0).start()

    def tails_of(tiles):
        return transposed_blocks([tile.astype(F32) for tile in tiles])

    for d in range(NZ):
        if d == 0:
            src = jbuf[0, 0, 0:64, :]
        else:
            z_copy(d).wait_recv()
            src = zbuf[d, 0:64, :]
        xi[:, d * LANES : (d + 1) * LANES] = extended(src.astype(F32), True).astype(BF16)
    for q in range(NZ // 4):
        tiles = [
            jbuf[0, 0, 64:80, :] if 4 * q + b == 0 else zbuf[4 * q + b, 64:80, :] for b in range(4)
        ]
        tile = jnp.concatenate(tails_of(tiles), axis=0)
        at = NZ * LANES + q * LANES
        xi[:, at : at + LANES] = extended(tile, True).astype(BF16)

    ones_row = (lax.broadcasted_iota(jnp.int32, (16, GROUP), 0) == 0).astype(F32).astype(BF16)

    def group_of(half, q):
        base = pl.multiple_of((half * 4 + q) * GROUP, GROUP)
        first = q * 4
        for b in range(4):
            src = jbuf[half, first + b, 0:64, :].astype(F32)
            xj[pl.ds(base + b * LANES, LANES), :] = extended(src, False).T.astype(BF16)
            panel[0:K, pl.ds(base + b * LANES, LANES)] = jbuf[half, first + b, 80:112, :]
        tile = jnp.concatenate(tails_of([jbuf[half, first + b, 64:80, :] for b in range(4)]), axis=0)
        xj[pl.ds(base + 4 * LANES, LANES), :] = extended(tile, False).T.astype(BF16)
        tile = tails_of([jbuf[half, first + b, 112:128, :] for b in range(4)])[0:2]
        panel[0:K, pl.ds(base + 4 * LANES, LANES)] = jnp.concatenate(tile, axis=0).astype(BF16)
        panel[K : K + 16, pl.ds(base, GROUP)] = ones_row
        for c in range(ROWS_I // 256):
            dist = jnp.dot(
                xj[pl.ds(base, GROUP), :],
                xi[:, c * 256 : (c + 1) * 256],
                preferred_element_type=F32,
            )
            weights = jnp.exp2(dist * (KERNEL_SCALE / F * math.log2(math.e)))
            aff[pl.ds(base, GROUP), c * 256 : (c + 1) * 256] = weights.astype(BF16)

    def direct(q, carry):
        for b in range(4):
            e = q * 4 + b

            @pl.when(e > 0)
            def _():
                xy_copy(e).wait_recv()
                forward(e).start()

        group_of(0, q)
        return carry

    def forwarded(q, carry):
        for b in range(4):
            forward(q * 4 + b).wait_recv()
        group_of(1, q)
        return carry

    lax.fori_loop(0, 4, direct, 0)
    lax.fori_loop(0, 4, forwarded, 0)

    def product(rows):
        acc[0:rows, :] = jnp.zeros((rows, ROWS_I), F32)

        def step(s, carry):
            at = pl.multiple_of(s * 2 * GROUP, 2 * GROUP)
            acc[0:rows, :] += jnp.dot(
                panel[0:rows, pl.ds(at, 2 * GROUP)],
                aff[pl.ds(at, 2 * GROUP), :],
                preferred_element_type=F32,
            )
            return carry

        lax.fori_loop(0, COLS_J // (2 * GROUP), step, 0)

    blocks8 = lane_block()

    def p_copy(it, d):
        return remote(
            psend.at[it, d], precv.at[it, d], p_s.at[it, d], p_r.at[it, d], z_peer(-d)
        )

    def reduce_product(it, with_degree):
        for q in range(NZ // 4):
            at = NZ * LANES + q * LANES
            tail = acc[0:K, at : at + LANES]
            if it == 1:
                tail = tail + acc[K : 2 * K, at : at + LANES]
            packed = [
                pick(blocks8, [roll_lanes(tail[8 * g : 8 * g + 8], TAIL * (g - b)) for g in range(4)])
                for b in range(4)
            ]
            for b in range(4):
                d = 4 * q + b
                main = acc[0:K, d * LANES : (d + 1) * LANES]
                if it == 1:
                    main = main + acc[K : 2 * K, d * LANES : (d + 1) * LANES]
                psend[it, d, 0:K, :] = main
                psend[it, d, K : K + 8, :] = packed[b]
                if with_degree:
                    psend[it, d, K + 8 : K + 9, :] = acc[K : K + 1, d * LANES : (d + 1) * LANES]
                    psend[it, d, K + 9 : K + 10, :] = roll_lanes(
                        acc[K : K + 8, at : at + LANES], -TAIL * b
                    )[0:1]
                    psend[it, d, K + 10 : K + 16, :] = jnp.zeros((6, LANES), F32)
                else:
                    psend[it, d, K + 8 : K + 16, :] = jnp.zeros((8, LANES), F32)
        for d in range(1, NZ):
            p_copy(it, d).start()
        total = psend[it, 0]
        for d in range(1, NZ):
            p_copy(it, d).wait_recv()
            total = total + precv[it, d]
        return total

    def gram_of(scaled):
        wide = jnp.concatenate([scaled, jnp.zeros((LANES - K, 2 * LANES), F32)], axis=0)
        part = lax.dot_general(
            scaled, wide, (((1,), (1,)), ((), ())), precision=HIGHEST, preferred_element_type=F32
        )
        return packed_tail(part, 8)

    def ga_copy(it, d):
        return remote(gsend.at[it, 0], grecv.at[it, 0, d], ga_s.at[it, d], ga_r.at[it, d], col_peer(d))

    def gb_copy(it, e):
        return remote(gsend.at[it, 1], grecv.at[it, 1, e], gb_s.at[it, e], gb_r.at[it, e], xy_peer(e))

    def gram_first(it, scaled):
        gsend[it, 0] = gram_of(scaled)
        for d in range(1, NCOL):
            ga_copy(it, d).start()

    def gram_second(it):
        total = gsend[it, 0]
        for d in range(1, NCOL):
            ga_copy(it, d).wait_recv()
            total = total + grecv[it, 0, d]
        gsend[it, 1] = total
        for e in range(1, NXY):
            gb_copy(it, e).start()

    def gram_last(it):
        total = gsend[it, 1]
        for e in range(1, NXY):
            gb_copy(it, e).wait_recv()
            total = total + grecv[it, 1, e]
        return unpacked_tail(total, 4) * (1.0 / TOTAL)

    def s_copy(e):
        return remote(sbuf.at[0, 0], sbuf.at[0, e], s_s.at[e], s_r.at[e], xy_peer(e))

    def s_forward(e):
        return remote(sbuf.at[0, e], sbuf.at[1, e], sf_s.at[e], sf_r.at[e], partner)

    product(K + 16)
    total = reduce_product(0, True)
    keep = lax.broadcasted_iota(jnp.int32, (K, LANES), 1) < TAIL
    deg_main = total[K + 8 : K + 9]
    deg_tail = jnp.where(keep[0:1], total[K + 9 : K + 10], 1.0)
    scaled_main = total[0:K] / deg_main
    scaled_tail = unpacked_tail(total[K : K + 8], 4) / deg_tail
    scaled = jnp.concatenate([scaled_main, scaled_tail], axis=1)

    hi = scaled.astype(BF16).astype(F32)
    lo = scaled - hi
    both = jnp.concatenate([hi, lo], axis=0)
    sbuf[0, 0, 0:64, :] = both[:, 0:LANES].astype(BF16)
    sbuf[0, 0, 64:80, :] = packed_tail(both[:, LANES:], 16).astype(BF16)
    for e in range(1, NXY):
        s_copy(e).start()
    s_forward(0).start()
    gram_first(0, scaled)
    for e in range(1, NXY):
        s_copy(e).wait_recv()
        s_forward(e).start()
    gram_second(0)

    def fill(half, q, carry):
        base = pl.multiple_of((half * 4 + q) * GROUP, GROUP)
        first = q * 4
        for b in range(4):
            panel[0 : 2 * K, pl.ds(base + b * LANES, LANES)] = sbuf[half, first + b, 0:64, :]
        tile = tails_of([sbuf[half, first + b, 64:80, :] for b in range(4)])
        panel[0 : 2 * K, pl.ds(base + 4 * LANES, LANES)] = jnp.concatenate(tile, axis=0).astype(BF16)
        return carry

    lax.fori_loop(0, 4, functools.partial(fill, 0), 0)
    for e in range(NXY):
        s_forward(e).wait_recv()
    lax.fori_loop(0, 4, functools.partial(fill, 1), 0)

    product(2 * K)
    eye = (
        lax.broadcasted_iota(jnp.int32, (K, LANES), 0)
        == lax.broadcasted_iota(jnp.int32, (K, LANES), 1)
    ).astype(F32)
    total = reduce_product(1, False)
    inverse = eliminate(gram_last(0), eye)
    scaled = jnp.concatenate([total[0:K] / deg_main, unpacked_tail(total[K : K + 8], 4) / deg_tail], axis=1)
    tall = jnp.concatenate([scaled, jnp.zeros((LANES - K, 2 * LANES), F32)], axis=0)
    scaled = jnp.dot(inverse, tall, precision=HIGHEST, preferred_element_type=F32)
    gram_first(1, scaled)
    gram_second(1)
    ortho = eliminate(gram_last(1), scaled)
    wide = jnp.concatenate([ortho, jnp.zeros((LANES - K, 2 * LANES), F32)], axis=0)
    out_ref[...] = wide.T[0:OWN, 0:K]

    for d in range(1, NZ):
        z_copy(d).wait_send()
        for it in range(2):
            p_copy(it, d).wait_send()
    for e in range(NXY):
        forward(e).wait_send()
        s_forward(e).wait_send()
    for e in range(1, NXY):
        xy_copy(e).wait_send()
        s_copy(e).wait_send()
        for it in range(2):
            ga_copy(it, e).wait_send()
            gb_copy(it, e).wait_send()


def solution(mesh):
    dma = pltpu.SemaphoreType.DMA

    def shards(points, start_vectors):
        return pl.pallas_call(
            kernel,
            out_shape=jax.ShapeDtypeStruct((OWN, K), F32),
            in_specs=[pl.BlockSpec(memory_space=pltpu.VMEM)] * 2,
            out_specs=pl.BlockSpec(memory_space=pltpu.VMEM),
            scratch_shapes=[
                pltpu.VMEM((2 * LANES, LANES), F32),
                pltpu.VMEM((NZ, 80, LANES), BF16),
                pltpu.VMEM((2, NXY, LANES, LANES), BF16),
                pltpu.VMEM((LANES, ROWS_I), BF16),
                pltpu.VMEM((COLS_J, LANES), BF16),
                pltpu.VMEM((2 * K, COLS_J), BF16),
                pltpu.VMEM((COLS_J, ROWS_I), BF16),
                pltpu.VMEM((2 * K, ROWS_I), F32),
                pltpu.VMEM((2, NZ, K + 16, LANES), F32),
                pltpu.VMEM((2, NZ, K + 16, LANES), F32),
                pltpu.VMEM((2, NXY, 80, LANES), BF16),
                pltpu.VMEM((2, 2, 8, LANES), F32),
                pltpu.VMEM((2, 2, 16, 8, LANES), F32),
                dma((NZ,)), dma((NZ,)),
                dma((NXY,)), dma((NXY,)),
                dma((NXY,)), dma((NXY,)),
                dma((2, NZ)), dma((2, NZ)),
                dma((NXY,)), dma((NXY,)),
                dma((NXY,)), dma((NXY,)),
                dma((2, NCOL)), dma((2, NCOL)),
                dma((2, NXY)), dma((2, NXY)),
            ],
            compiler_params=pltpu.CompilerParams(
                collective_id=0, has_side_effects=True, vmem_limit_bytes=48 * 1024 * 1024
            ),
        )(points, start_vectors)

    spec = P(("row", "col"), None)
    return jax.shard_map(
        shards, mesh=mesh, in_specs=(spec, spec), out_specs=spec, check_vma=False
    )
```

time: 277 us -> 68.2 us (0.25)
  the two profiles are of different devices: /device:TPU:32 before, /device:TPU:1 now
where the time goes in v1:
time: 68.2 us; the launch traced here: 68 us
  Pallas kernels  66.3 us (97%)
  local copies, waits for them, and re-layouts  1.69 us (2%)
    pallas_call x1, Pallas kernels, shards(): pl.pallas_call(kernel, out_shape=jax.ShapeDtypeStruct((OWN, K), F32), in_...  66.3 us

profile of v1, /device:TPU:1, one launch (start us, length us, event | category | flops | bytes accessed | tf_op | source)
XLA Modules:
  0.0 68.0 jit_solution(11126156999951328043)
XLA Ops:
  0.0 0.0 copy-start
  0.0 0.9 %copy.3.pts_ref = bf16[160,64]{1,0:T(8,128)(2,1)S(1)} copy(bf16[160,64]{0,1:T(8,128)(2,1)} %param.2) | data formatting | bytes 40960 | tf_op args[0]
  0.9 0.0 copy-done
  0.9 0.1 copy.4.vec_ref
  1.0 66.3 %shard_map.28 = f32[160,32]{1,0:T(8,128)S(1)} custom-call(bf16[160,64]{1,0:T(8,128)(2,1)S(1)} %copy.3.pts_ref, bf16[160,32]{1,0:T(8,128)(2,1)S(1)} %copy.4.vec_ref), custom_call_target="tpu_custom_call" | custom-call | tf_op jit(solution)/shard_map/pallas_call | solution.py:422
  67.3 0.7 %copy.5 = f32[160,32]{0,1:T(8,128)} copy(f32[160,32]{1,0:T(8,128)S(1)} %shard_map.28) | data formatting | bytes 40960 | tf_op jit(solution)/shard_map/pallas_call | solution.py:422
Async XLA Ops:
  0.0 0.9 %copy-start = (bf16[160,32]{0,1:T(8,128)(2,1)S(1)}, bf16[160,32]{0,1:T(8,128)(2,1)}, u32[]{:S(2)}) copy-start(bf16[160,32]{0,1:T(8,128)(2,1)} %param.3) | copy-start | bytes 30724

commit v2 on v1

v2 whole, which is shorter than its diff:
```python
import functools
import math

import jax
import jax.numpy as jnp
from jax import lax
from jax.experimental import pallas as pl
from jax.experimental.pallas import tpu as pltpu
from jax.sharding import PartitionSpec as P

MESH = pl.DeviceIdType.MESH
F32 = jnp.float32
BF16 = jnp.bfloat16
HIGHEST = lax.Precision.HIGHEST

KERNEL_SCALE = 5.12
F = 64
K = 32
OWN = 160
LANES = 128
TAIL = OWN - LANES
GROUP = 4 * OWN
NZ = 8
NX = 4
NY = 4
NXY = NX * NY
NCOL = 2 * NZ
ROWS_I = NZ * OWN
COLS_J = 2 * NXY * OWN
TOTAL = 256 * OWN


def lane_block():
    return lax.broadcasted_iota(jnp.int32, (8, LANES), 1) // TAIL


def roll_lanes(x, shift):
    shift = shift % LANES
    return x if shift == 0 else pltpu.roll(x, shift, 1)


def pick(blocks, pieces):
    out = pieces[3]
    for b in (2, 1, 0):
        out = jnp.where(blocks == b, pieces[b], out)
    return out


def transposed_blocks(tiles):
    rows = tiles[0].shape[0]
    blocks = lax.broadcasted_iota(jnp.int32, (rows, LANES), 1) // TAIL
    return [
        pick(blocks, [roll_lanes(tiles[b], TAIL * (b - g)) for b in range(4)]) for g in range(4)
    ]


def packed_tail(tail, rows):
    groups = tail.shape[0] // rows
    return sum(roll_lanes(tail[g * rows : (g + 1) * rows], TAIL * g) for g in range(groups))


def unpacked_tail(packed, groups):
    rows = packed.shape[0]
    keep = lax.broadcasted_iota(jnp.int32, (rows, LANES), 1) < TAIL
    return jnp.concatenate(
        [jnp.where(keep, roll_lanes(packed, -TAIL * g), 0.0) for g in range(groups)], axis=0
    )


def bf16_pieces(x):
    hi = x.astype(BF16).astype(F32)
    rest = x - hi
    mid = rest.astype(BF16).astype(F32)
    return hi, mid, rest - mid


def extended(x, for_rows):
    hi, mid, lo = bf16_pieces(jnp.sum(x * x, axis=0, keepdims=True))
    r = lax.broadcasted_iota(jnp.int32, (8, LANES), 0)
    if for_rows:
        x = 2.0 * x
        head = jnp.where(r == 3, -hi, jnp.where(r == 4, -mid, jnp.where(r == 5, -lo, 0.0)))
        extra = jnp.where(r < 3, -1.0, head)
    else:
        head = jnp.where(r == 0, hi, jnp.where(r == 1, mid, jnp.where(r == 2, lo, 0.0)))
        extra = jnp.where((r >= 3) & (r < 6), 1.0, head)
    return jnp.concatenate([x, extra, jnp.zeros((LANES - F - 8, LANES), F32)], axis=0)


def eliminate(gram, right):
    cols = [jnp.broadcast_to(gram[:, m : m + 1], (K, LANES)) for m in range(K)]
    width = right.shape[1] // LANES
    sub = lax.broadcasted_iota(jnp.int32, (8, LANES), 0)
    cols = [[c[8 * g : 8 * g + 8] for g in range(4)] for c in cols]
    rt = [
        [right[8 * g : 8 * g + 8, w * LANES : (w + 1) * LANES] for w in range(width)]
        for g in range(4)
    ]
    out_rows = []
    for k in range(K):
        kg, kr = k // 8, k % 8
        pivot = cols[k][kg][kr : kr + 1]
        inv = 1.0 / pivot
        factor = [None] * 4
        for g in range(kg, 4):
            f = cols[k][g] * inv
            if g == kg:
                f = jnp.where(sub > kr, f, 0.0)
            factor[g] = f
        for m in range(k + 1, K):
            mg, mr = m // 8, m % 8
            upper = cols[k][mg][mr : mr + 1]
            for g in range(mg, 4):
                cols[m][g] = cols[m][g] - factor[g] * upper
        rows = [rt[kg][w][kr : kr + 1] for w in range(width)]
        scale = lax.rsqrt(pivot)
        out_rows.append([row * scale for row in rows])
        for g in range(kg, 4):
            for w in range(width):
                rt[g][w] = rt[g][w] - factor[g] * rows[w]
    tiles = []
    for g in range(4):
        tile = []
        for w in range(width):
            acc = jnp.broadcast_to(out_rows[8 * g][w], (8, LANES))
            for r in range(1, 8):
                acc = jnp.where(sub == r, out_rows[8 * g + r][w], acc)
            tile.append(acc)
        tiles.append(jnp.concatenate(tile, axis=1) if width > 1 else tile[0])
    return jnp.concatenate(tiles, axis=0)


def kernel(
    pts_hbm, vec_hbm, out_ref,
    pts_ref, vec_ref, stage, zbuf, jbuf, vbuf, xi, xj, panel, aff, acc, psend, precv, sbuf, gsend, grecv,
    in_s, z_s, z_r, xy_s, xy_r, f_s, f_r, v_s, v_r, vf_s, vf_r,
    p_s, p_r, s_s, s_r, sf_s, sf_r, ga_s, ga_r, gb_s, gb_r,
):
    row = lax.axis_index("row")
    col = lax.axis_index("col")
    x, y = row // NY, lax.rem(row, NY)
    z, core = col // 2, lax.rem(col, 2)

    def xy_peer(e):
        q = e // NY
        to_x = lax.rem(x + q + (q // 2) * (5 - 2 * q), NX)
        to_y = lax.rem(y + e % NY, NY)
        return (to_x * NY + to_y, col)

    def z_peer(d):
        return (row, lax.rem(z + d + NZ, NZ) * 2 + core)

    def col_peer(d):
        return (row, lax.rem(col + d, NCOL))

    partner = (row, z * 2 + 1 - core)

    def remote(src, dst, send, recv, to):
        return pltpu.make_async_remote_copy(
            src_ref=src, dst_ref=dst, send_sem=send, recv_sem=recv,
            device_id=to, device_id_type=MESH,
        )

    pts_copy = pltpu.make_async_copy(pts_hbm, pts_ref, in_s.at[0])
    vec_copy = pltpu.make_async_copy(vec_hbm, vec_ref, in_s.at[1])
    pts_copy.start()
    vec_copy.start()
    barrier = pltpu.get_barrier_semaphore()
    with jax.named_scope("signal"):
        for d in range(1, NCOL):
            pl.semaphore_signal(barrier, inc=1, device_id=col_peer(d), device_id_type=MESH)
        for e in range(1, NXY):
            pl.semaphore_signal(barrier, inc=1, device_id=xy_peer(e), device_id_type=MESH)

    with jax.named_scope("prepare"):
        stage[...] = jnp.zeros_like(stage)
        pts_copy.wait()
        vec_copy.wait()
        stage[0:F, 0:OWN] = pts_ref[...].astype(F32)
        stage[F : F + K, 0:OWN] = vec_ref[...].astype(F32)
        t = stage[...]
        jbuf[0, 0, 0:64, :] = t[0:F, 0:LANES].astype(BF16)
        jbuf[0, 0, 64:80, :] = packed_tail(t[0:F, LANES:], 16).astype(BF16)
        vbuf[0, 0, 0:32, :] = t[F : F + K, 0:LANES].astype(BF16)
        vbuf[0, 0, 32:48, :] = packed_tail(t[F : F + K, LANES:], 16).astype(BF16)
        acc[...] = jnp.zeros_like(acc)
        for h in range(COLS_J // GROUP):
            panel[K : K + 16, h * GROUP : (h + 1) * GROUP] = (
                lax.broadcasted_iota(jnp.int32, (16, GROUP), 0) == 0
            ).astype(F32).astype(BF16)

    with jax.named_scope("barrier_wait"):
        pl.semaphore_wait(barrier, NCOL - 1 + NXY - 1)

    def z_copy(d):
        return remote(jbuf.at[0, 0], zbuf.at[d], z_s.at[d], z_r.at[d], z_peer(d))

    def xy_copy(e):
        return remote(jbuf.at[0, 0], jbuf.at[0, e], xy_s.at[e], xy_r.at[e], xy_peer(e))

    def forward(e):
        return remote(jbuf.at[0, e], jbuf.at[1, e], f_s.at[e], f_r.at[e], partner)

    def v_copy(e):
        return remote(vbuf.at[0, 0], vbuf.at[0, e], v_s.at[e], v_r.at[e], xy_peer(e))

    def v_forward(e):
        return remote(vbuf.at[0, e], vbuf.at[1, e], vf_s.at[e], vf_r.at[e], partner)

    def s_copy(e):
        return remote(sbuf.at[0, 0], sbuf.at[0, e], s_s.at[e], s_r.at[e], xy_peer(e))

    def s_forward(e):
        return remote(sbuf.at[0, e], sbuf.at[1, e], sf_s.at[e], sf_r.at[e], partner)

    def pass_on(q, copies):
        for copy, onward in copies:
            for b in range(4):
                e = q * 4 + b

                if isinstance(q, int):
                    if e > 0:
                        copy(e).wait_recv()
                    onward(e).start()
                else:
                    copy(e).wait_recv()
                    onward(e).start()

    def in_groups(copies, work, name):
        with jax.named_scope(name + "_first"):
            pass_on(0, copies)

        def step(q, carry):
            with jax.named_scope(name + "_wait"):
                pass_on(q + 1, copies)
                for _, onward in copies:
                    for b in range(4):
                        onward(q * 4 + b).wait_recv()
            with jax.named_scope(name + "_work"):
                work(q)
            return carry

        lax.fori_loop(0, 3, step, 0)
        with jax.named_scope(name + "_lastwait"):
            for _, onward in copies:
                for b in range(4):
                    onward(12 + b).wait_recv()
        with jax.named_scope(name + "_lastwork"):
            work(3)

    with jax.named_scope("send_points"):
        for d in (4, 3, 5, 2, 6, 1, 7):
            z_copy(d).start()
        for e in range(1, NXY):
            xy_copy(e).start()
        for e in range(1, NXY):
            v_copy(e).start()

    def tails_of(tiles):
        return transposed_blocks([tile.astype(F32) for tile in tiles])

    with jax.named_scope("row_side"):
        for d in range(NZ):
            if d == 0:
                src = jbuf[0, 0, 0:64, :]
            else:
                z_copy(d).wait_recv()
                src = zbuf[d, 0:64, :]
            xi[:, d * LANES : (d + 1) * LANES] = extended(src.astype(F32), True).astype(BF16)
        for q in range(NZ // 4):
            tiles = [
                jbuf[0, 0, 64:80, :] if 4 * q + b == 0 else zbuf[4 * q + b, 64:80, :]
                for b in range(4)
            ]
            tile = jnp.concatenate(tails_of(tiles), axis=0)
            at = NZ * LANES + q * LANES
            xi[:, at : at + LANES] = extended(tile, True).astype(BF16)

    def first_work(q):
        base = pl.multiple_of(q * 2 * GROUP, 2 * GROUP)
        for half in range(2):
            for b in range(4):
                e = q * 4 + b
                at = half * GROUP + b * LANES
                src = jbuf[half, e, 0:64, :].astype(F32)
                xj[at : at + LANES, :] = extended(src, False).T.astype(BF16)
                panel[0:K, pl.ds(base + at, LANES)] = vbuf[half, e, 0:32, :]
            at = half * GROUP + 4 * LANES
            tile = tails_of([jbuf[half, q * 4 + b, 64:80, :] for b in range(4)])
            xj[at : at + LANES, :] = extended(jnp.concatenate(tile, axis=0), False).T.astype(BF16)
            tile = tails_of([vbuf[half, q * 4 + b, 32:48, :] for b in range(4)])[0:2]
            panel[0:K, pl.ds(base + at, LANES)] = jnp.concatenate(tile, axis=0).astype(BF16)
        vectors = panel[0 : K + 16, pl.ds(base, 2 * GROUP)]
        for c in range(ROWS_I // 256):
            here = slice(c * 256, (c + 1) * 256)
            dist = jnp.dot(xj[...], xi[:, here], preferred_element_type=F32)
            weights = jnp.exp2(dist * (KERNEL_SCALE / F * math.log2(math.e))).astype(BF16)
            aff[pl.ds(base, 2 * GROUP), here] = weights
            acc[0 : K + 16, here] += jnp.dot(vectors, weights, preferred_element_type=F32)

    in_groups([(xy_copy, forward), (v_copy, v_forward)], first_work, "a")

    blocks8 = lane_block()

    def p_copy(it, d):
        rows = K + 16 - 8 * it
        return remote(
            psend.at[it, d, pl.ds(0, rows)], precv.at[it, d, pl.ds(0, rows)],
            p_s.at[it, d], p_r.at[it, d], z_peer(-d),
        )

    def send_product(it):
        for q in range(NZ // 4):
            at = NZ * LANES + q * LANES
            tail = acc[0:K, at : at + LANES]
            if it == 1:
                tail = tail + acc[K : 2 * K, at : at + LANES]
            packed = [
                pick(blocks8, [roll_lanes(tail[8 * g : 8 * g + 8], TAIL * (g - b)) for g in range(4)])
                for b in range(4)
            ]
            for b in range(4):
                d = 4 * q + b
                main = acc[0:K, d * LANES : (d + 1) * LANES]
                if it == 1:
                    main = main + acc[K : 2 * K, d * LANES : (d + 1) * LANES]
                psend[it, d, 0:K, :] = main
                psend[it, d, K : K + 8, :] = packed[b]
                if it == 0:
                    psend[it, d, K + 8 : K + 9, :] = acc[K : K + 1, d * LANES : (d + 1) * LANES]
                    psend[it, d, K + 9 : K + 10, :] = roll_lanes(
                        acc[K : K + 8, at : at + LANES], -TAIL * b
                    )[0:1]
                    psend[it, d, K + 10 : K + 16, :] = jnp.zeros((6, LANES), F32)
        for d in (4, 3, 5, 2, 6, 1, 7):
            p_copy(it, d).start()

    def received_product(it):
        rows = K + 16 - 8 * it
        total = psend[it, 0, 0:rows]
        for d in (1, 7, 2, 6, 3, 5, 4):
            p_copy(it, d).wait_recv()
            total = total + precv[it, d, 0:rows]
        return total

    def gram_of(scaled):
        wide = jnp.concatenate([scaled, jnp.zeros((LANES - K, 2 * LANES), F32)], axis=0)
        part = lax.dot_general(
            scaled, wide, (((1,), (1,)), ((), ())), precision=HIGHEST, preferred_element_type=F32
        )
        return packed_tail(part, 8)

    def ga_copy(it, d):
        return remote(gsend.at[it, 0], grecv.at[it, 0, d], ga_s.at[it, d], ga_r.at[it, d], col_peer(d))

    def gb_copy(it, e):
        return remote(gsend.at[it, 1], grecv.at[it, 1, e], gb_s.at[it, e], gb_r.at[it, e], xy_peer(e))

    def gram_first(it, scaled):
        gsend[it, 0] = gram_of(scaled)
        for d in range(1, NCOL):
            ga_copy(it, d).start()

    def gram_second(it):
        total = gsend[it, 0]
        for d in range(1, NCOL):
            ga_copy(it, d).wait_recv()
            total = total + grecv[it, 0, d]
        gsend[it, 1] = total
        for e in range(1, NXY):
            gb_copy(it, e).start()

    def gram_last(it):
        total = gsend[it, 1]
        for e in range(1, NXY):
            gb_copy(it, e).wait_recv()
            total = total + grecv[it, 1, e]
        return unpacked_tail(total, 4) * (1.0 / TOTAL)

    with jax.named_scope("send1"):
        send_product(0)
    with jax.named_scope("reduce1"):
        total = received_product(0)
    with jax.named_scope("scale1"):
        keep = lax.broadcasted_iota(jnp.int32, (1, LANES), 1) < TAIL
        deg_main = total[K + 8 : K + 9]
        deg_tail = jnp.where(keep, total[K + 9 : K + 10], 1.0)
        scaled_main = total[0:K] / deg_main
        scaled_tail = unpacked_tail(total[K : K + 8], 4) / deg_tail
        scaled = jnp.concatenate([scaled_main, scaled_tail], axis=1)

        hi = scaled.astype(BF16).astype(F32)
        lo = scaled - hi
        both = jnp.concatenate([hi, lo], axis=0)
        sbuf[0, 0, 0:64, :] = both[:, 0:LANES].astype(BF16)
        sbuf[0, 0, 64:80, :] = packed_tail(both[:, LANES:], 16).astype(BF16)
        for e in range(1, NXY):
            s_copy(e).start()
    with jax.named_scope("gram_first1"):
        gram_first(0, scaled)
        acc[...] = jnp.zeros_like(acc)

    def second_work(q):
        base = pl.multiple_of(q * 2 * GROUP, 2 * GROUP)
        for half in range(2):
            for b in range(4):
                at = base + half * GROUP + b * LANES
                panel[0 : 2 * K, pl.ds(at, LANES)] = sbuf[half, q * 4 + b, 0:64, :]
            tile = tails_of([sbuf[half, q * 4 + b, 64:80, :] for b in range(4)])
            at = base + half * GROUP + 4 * LANES
            panel[0 : 2 * K, pl.ds(at, LANES)] = jnp.concatenate(tile, axis=0).astype(BF16)
        acc[...] += jnp.dot(
            panel[:, pl.ds(base, 2 * GROUP)],
            aff[pl.ds(base, 2 * GROUP), :],
            preferred_element_type=F32,
        )

    in_groups([(s_copy, s_forward)], second_work, "b")

    eye = (
        lax.broadcasted_iota(jnp.int32, (K, LANES), 0)
        == lax.broadcasted_iota(jnp.int32, (K, LANES), 1)
    ).astype(F32)
    with jax.named_scope("send2"):
        send_product(1)
    with jax.named_scope("gram_second1"):
        gram_second(0)
    with jax.named_scope("gram_last1"):
        last = gram_last(0)
    with jax.named_scope("eliminate1"):
        inverse = eliminate(last, eye)
    with jax.named_scope("reduce2"):
        total = received_product(1)
    with jax.named_scope("scale2"):
        scaled = jnp.concatenate(
            [total[0:K] / deg_main, unpacked_tail(total[K : K + 8], 4) / deg_tail], axis=1
        )
        tall = jnp.concatenate([scaled, jnp.zeros((LANES - K, 2 * LANES), F32)], axis=0)
        scaled = jnp.dot(inverse, tall, precision=HIGHEST, preferred_element_type=F32)
    with jax.named_scope("gram_first2"):
        gram_first(1, scaled)
    with jax.named_scope("gram_second2"):
        gram_second(1)
    with jax.named_scope("gram_last2"):
        last = gram_last(1)
    with jax.named_scope("eliminate2"):
        ortho = eliminate(last, scaled)
        out_ref[...] = ortho[:, 0:OWN]

    for d in range(1, NZ):
        z_copy(d).wait_send()
        for it in range(2):
            p_copy(it, d).wait_send()
    for e in range(NXY):
        forward(e).wait_send()
        v_forward(e).wait_send()
        s_forward(e).wait_send()
    for e in range(1, NXY):
        xy_copy(e).wait_send()
        v_copy(e).wait_send()
        s_copy(e).wait_send()
        for it in range(2):
            ga_copy(it, e).wait_send()
            gb_copy(it, e).wait_send()


def solution(mesh):
    dma = pltpu.SemaphoreType.DMA

    def shards(points, start_vectors):
        return pl.pallas_call(
            kernel,
            out_shape=jax.ShapeDtypeStruct((K, OWN), F32),
            in_specs=[pl.BlockSpec(memory_space=pltpu.HBM)] * 2,
            out_specs=pl.BlockSpec(memory_space=pltpu.VMEM),
            scratch_shapes=[
                pltpu.VMEM((F, OWN), BF16),
                pltpu.VMEM((K, OWN), BF16),
                pltpu.VMEM((F + K, 2 * LANES), F32),
                pltpu.VMEM((NZ, 80, LANES), BF16),
                pltpu.VMEM((2, NXY, 80, LANES), BF16),
                pltpu.VMEM((2, NXY, 48, LANES), BF16),
                pltpu.VMEM((LANES, ROWS_I), BF16),
                pltpu.VMEM((2 * GROUP, LANES), BF16),
                pltpu.VMEM((2 * K, COLS_J), BF16),
                pltpu.VMEM((COLS_J, ROWS_I), BF16),
                pltpu.VMEM((2 * K, ROWS_I), F32),
                pltpu.VMEM((2, NZ, K + 16, LANES), F32),
                pltpu.VMEM((2, NZ, K + 16, LANES), F32),
                pltpu.VMEM((2, NXY, 80, LANES), BF16),
                pltpu.VMEM((2, 2, 8, LANES), F32),
                pltpu.VMEM((2, 2, 16, 8, LANES), F32),
                dma((2,)),
                dma((NZ,)), dma((NZ,)),
                dma((NXY,)), dma((NXY,)),
                dma((NXY,)), dma((NXY,)),
                dma((NXY,)), dma((NXY,)),
                dma((NXY,)), dma((NXY,)),
                dma((2, NZ)), dma((2, NZ)),
                dma((NXY,)), dma((NXY,)),
                dma((NXY,)), dma((NXY,)),
                dma((2, NCOL)), dma((2, NCOL)),
                dma((2, NXY)), dma((2, NXY)),
            ],
            compiler_params=pltpu.CompilerParams(
                collective_id=0, has_side_effects=True, vmem_limit_bytes=48 * 1024 * 1024
            ),
        )(points.T, start_vectors.T).T

    spec = P(("row", "col"), None)
    return jax.shard_map(
        shards, mesh=mesh, in_specs=(spec, spec), out_specs=spec, check_vma=False
    )
```

time: 68.2 us -> 68.5 us (level)
    unnamed x4 -> x5, local copies, waits for them, and re-layouts: 0.99 us -> 2.09 us
    pallas_call x1 -> x0, local copies, waits for them, and re-layouts: 0.69 us -> none  [shards(): pl.pallas_call(kernel, out_shape=jax.ShapeDtypeStruct((OWN, K), F32), in_...]
where the time goes in v2:
time: 68.5 us; the launch traced here: 68.3 us
  Pallas kernels  66.2 us (97%)
  local copies, waits for them, and re-layouts  2.09 us (3%)
    pallas_call x1, Pallas kernels, shards(): pl.pallas_call(kernel, out_shape=jax.ShapeDtypeStruct((K, OWN), F32), in_...  66.2 us
    unnamed x5, local copies, waits for them, and re-layouts  2.09 us

profile of v2, /device:TPU:1, one launch (start us, length us, event | category | flops | bytes accessed | tf_op | source)
XLA Modules:
  0.0 68.3 jit_solution(376304405871532701)
XLA Ops:
  0.0 0.0 copy-start
  0.0 0.8 %copy-done = bf16[160,64]{0,1:T(8,128)(2,1)S(1)} copy-done((bf16[160,64]{0,1:T(8,128)(2,1)S(1)}, bf16[160,64]{0,1:T(8,128)(2,1)}, u32[]{:S(2)}) %copy-start) | copy-done | bytes 20504
  0.8 0.0 copy-start.1
  0.8 0.7 %copy-done.1 = bf16[160,32]{0,1:T(8,128)(2,1)S(1)} copy-done((bf16[160,32]{0,1:T(8,128)(2,1)S(1)}, bf16[160,32]{0,1:T(8,128)(2,1)}, u32[]{:S(2)}) %copy-start.1) | copy-done | bytes 10264
  1.5 66.2 %shard_map.28 = f32[32,160]{1,0:T(8,128)S(1)} custom-call(bf16[64,160]{1,0:T(8,128)(2,1)S(1)} %bitcast.4, bf16[32,160]{1,0:T(8,128)(2,1)S(1)} %bitcast.5), custom_call_target="tpu_custom_call" | custom-call | tf_op jit(solution)/shard_map/pallas_call | solution.py:471
  67.7 0.6 copy.4
Async XLA Ops:
  0.0 0.8 %copy-start = (bf16[160,64]{0,1:T(8,128)(2,1)S(1)}, bf16[160,64]{0,1:T(8,128)(2,1)}, u32[]{:S(2)}) copy-start(bf16[160,64]{0,1:T(8,128)(2,1)} %param.2) | copy-start | bytes 61444
  0.8 0.7 %copy-start.1 = (bf16[160,32]{0,1:T(8,128)(2,1)S(1)}, bf16[160,32]{0,1:T(8,128)(2,1)}, u32[]{:S(2)}) copy-start(bf16[160,32]{0,1:T(8,128)(2,1)} %param.3) | copy-start | bytes 30724

commit v3 on v2

--- a/solution.py
+++ b/solution.py
@@ -226,7 +226,7 @@
                     copy(e).wait_recv()
                     onward(e).start()
 
-    def in_groups(copies, work, name):
+    def in_groups(copies, work, name, before_last=None):
         with jax.named_scope(name + "_first"):
             pass_on(0, copies)
 
@@ -241,6 +241,8 @@
             return carry
 
         lax.fori_loop(0, 3, step, 0)
+        if before_last is not None:
+            before_last()
         with jax.named_scope(name + "_lastwait"):
             for _, onward in copies:
                 for b in range(4):
@@ -290,13 +292,18 @@
             xj[at : at + LANES, :] = extended(jnp.concatenate(tile, axis=0), False).T.astype(BF16)
             tile = tails_of([vbuf[half, q * 4 + b, 32:48, :] for b in range(4)])[0:2]
             panel[0:K, pl.ds(base + at, LANES)] = jnp.concatenate(tile, axis=0).astype(BF16)
-        vectors = panel[0 : K + 16, pl.ds(base, 2 * GROUP)]
         for c in range(ROWS_I // 256):
             here = slice(c * 256, (c + 1) * 256)
             dist = jnp.dot(xj[...], xi[:, here], preferred_element_type=F32)
-            weights = jnp.exp2(dist * (KERNEL_SCALE / F * math.log2(math.e))).astype(BF16)
-            aff[pl.ds(base, 2 * GROUP), here] = weights
-            acc[0 : K + 16, here] += jnp.dot(vectors, weights, preferred_element_type=F32)
+            weights = jnp.exp2(dist * (KERNEL_SCALE / F * math.log2(math.e)))
+            aff[pl.ds(base, 2 * GROUP), here] = weights.astype(BF16)
+        for c in range(ROWS_I // 256):
+            here = slice(c * 256, (c + 1) * 256)
+            acc[0 : K + 16, here] += jnp.dot(
+                panel[0 : K + 16, pl.ds(base, 2 * GROUP)],
+                aff[pl.ds(base, 2 * GROUP), here],
+                preferred_element_type=F32,
+            )
 
     in_groups([(xy_copy, forward), (v_copy, v_forward)], first_work, "a")
 
@@ -415,7 +422,7 @@
             preferred_element_type=F32,
         )
 
-    in_groups([(s_copy, s_forward)], second_work, "b")
+    in_groups([(s_copy, s_forward)], second_work, "b", lambda: gram_second(0))
 
     eye = (
         lax.broadcasted_iota(jnp.int32, (K, LANES), 0)
@@ -423,8 +430,6 @@
     ).astype(F32)
     with jax.named_scope("send2"):
         send_product(1)
-    with jax.named_scope("gram_second1"):
-        gram_second(0)
     with jax.named_scope("gram_last1"):
         last = gram_last(0)
     with jax.named_scope("eliminate1"):

time: 68.5 us -> 65 us (0.949)
  Pallas kernels: 66.2 us -> 62.7 us
    pallas_call x1, Pallas kernels: 66.2 us -> 62.7 us  [shards(): pl.pallas_call(kernel, out_shape=jax.ShapeDtypeStruct((K, OWN), F32), in_...]
where the time goes in v3:
time: 65 us; the launch traced here: 64.9 us
  Pallas kernels  62.7 us (96%)
  local copies, waits for them, and re-layouts  2.09 us (3%)
    pallas_call x1, Pallas kernels, shards(): pl.pallas_call(kernel, out_shape=jax.ShapeDtypeStruct((K, OWN), F32), in_...  62.7 us
    unnamed x5, local copies, waits for them, and re-layouts  2.09 us

profile of v3, /device:TPU:1, one launch (start us, length us, event | category | flops | bytes accessed | tf_op | source)
XLA Modules:
  0.0 64.9 jit_solution(11990416119084088339)
XLA Ops:
  0.0 0.0 copy-start
  0.0 0.8 %copy-done = bf16[160,64]{0,1:T(8,128)(2,1)S(1)} copy-done((bf16[160,64]{0,1:T(8,128)(2,1)S(1)}, bf16[160,64]{0,1:T(8,128)(2,1)}, u32[]{:S(2)}) %copy-start) | copy-done | bytes 20504
  0.8 0.0 copy-start.1
  0.8 0.7 %copy-done.1 = bf16[160,32]{0,1:T(8,128)(2,1)S(1)} copy-done((bf16[160,32]{0,1:T(8,128)(2,1)S(1)}, bf16[160,32]{0,1:T(8,128)(2,1)}, u32[]{:S(2)}) %copy-start.1) | copy-done | bytes 10264
  1.5 62.7 %shard_map.28 = f32[32,160]{1,0:T(8,128)S(1)} custom-call(bf16[64,160]{1,0:T(8,128)(2,1)S(1)} %bitcast.4, bf16[32,160]{1,0:T(8,128)(2,1)S(1)} %bitcast.5), custom_call_target="tpu_custom_call" | custom-call | tf_op jit(solution)/shard_map/pallas_call | solution.py:476
  64.2 0.6 copy.4
Async XLA Ops:
  0.0 0.8 %copy-start = (bf16[160,64]{0,1:T(8,128)(2,1)S(1)}, bf16[160,64]{0,1:T(8,128)(2,1)}, u32[]{:S(2)}) copy-start(bf16[160,64]{0,1:T(8,128)(2,1)} %param.2) | copy-start | bytes 61444
  0.8 0.7 %copy-start.1 = (bf16[160,32]{0,1:T(8,128)(2,1)S(1)}, bf16[160,32]{0,1:T(8,128)(2,1)}, u32[]{:S(2)}) copy-start(bf16[160,32]{0,1:T(8,128)(2,1)} %param.3) | copy-start | bytes 30724

commit v4 on v3

--- a/solution.py
+++ b/solution.py
@@ -14,6 +14,7 @@
 HIGHEST = lax.Precision.HIGHEST
 
 KERNEL_SCALE = 5.12
+WIDE = 1
 F = 64
 K = 32
 OWN = 160
@@ -28,10 +29,6 @@
 ROWS_I = NZ * OWN
 COLS_J = 2 * NXY * OWN
 TOTAL = 256 * OWN
-
-
-def lane_block():
-    return lax.broadcasted_iota(jnp.int32, (8, LANES), 1) // TAIL
 
 
 def roll_lanes(x, shift):
@@ -213,53 +210,33 @@
     def s_forward(e):
         return remote(sbuf.at[0, e], sbuf.at[1, e], sf_s.at[e], sf_r.at[e], partner)
 
-    def pass_on(q, copies):
-        for copy, onward in copies:
-            for b in range(4):
-                e = q * 4 + b
-
-                if isinstance(q, int):
-                    if e > 0:
-                        copy(e).wait_recv()
-                    onward(e).start()
-                else:
-                    copy(e).wait_recv()
-                    onward(e).start()
-
-    def in_groups(copies, work, name, before_last=None):
-        with jax.named_scope(name + "_first"):
-            pass_on(0, copies)
-
-        def step(q, carry):
-            with jax.named_scope(name + "_wait"):
-                pass_on(q + 1, copies)
-                for _, onward in copies:
-                    for b in range(4):
-                        onward(q * 4 + b).wait_recv()
-            with jax.named_scope(name + "_work"):
-                work(q)
-            return carry
-
-        lax.fori_loop(0, 3, step, 0)
-        if before_last is not None:
-            before_last()
-        with jax.named_scope(name + "_lastwait"):
-            for _, onward in copies:
-                for b in range(4):
-                    onward(12 + b).wait_recv()
-        with jax.named_scope(name + "_lastwork"):
-            work(3)
+    def arrived(q, copy, onward):
+        for b in range(4):
+            e = q * 4 + b
+            if isinstance(e, int) and e == 0:
+                continue
+            copy(e).wait_recv()
+            onward(e).start()
+
+    def forwarded(q, onward):
+        for b in range(4):
+            onward(q * 4 + b).wait_recv()
 
     with jax.named_scope("send_points"):
         for d in (4, 3, 5, 2, 6, 1, 7):
             z_copy(d).start()
         for e in range(1, NXY):
             xy_copy(e).start()
+        forward(0).start()
         for e in range(1, NXY):
             v_copy(e).start()
+        v_forward(0).start()
 
     def tails_of(tiles):
         return transposed_blocks([tile.astype(F32) for tile in tiles])
+
+    with jax.named_scope("first_points"):
+        arrived(0, xy_copy, forward)
 
     with jax.named_scope("row_side"):
         for d in range(NZ):
@@ -278,77 +255,110 @@
             at = NZ * LANES + q * LANES
             xi[:, at : at + LANES] = extended(tile, True).astype(BF16)
 
-    def first_work(q):
+    def affinity(q):
         base = pl.multiple_of(q * 2 * GROUP, 2 * GROUP)
         for half in range(2):
             for b in range(4):
-                e = q * 4 + b
                 at = half * GROUP + b * LANES
-                src = jbuf[half, e, 0:64, :].astype(F32)
+                src = jbuf[half, q * 4 + b, 0:64, :].astype(F32)
                 xj[at : at + LANES, :] = extended(src, False).T.astype(BF16)
-                panel[0:K, pl.ds(base + at, LANES)] = vbuf[half, e, 0:32, :]
             at = half * GROUP + 4 * LANES
             tile = tails_of([jbuf[half, q * 4 + b, 64:80, :] for b in range(4)])
             xj[at : at + LANES, :] = extended(jnp.concatenate(tile, axis=0), False).T.astype(BF16)
-            tile = tails_of([vbuf[half, q * 4 + b, 32:48, :] for b in range(4)])[0:2]
-            panel[0:K, pl.ds(base + at, LANES)] = jnp.concatenate(tile, axis=0).astype(BF16)
         for c in range(ROWS_I // 256):
             here = slice(c * 256, (c + 1) * 256)
             dist = jnp.dot(xj[...], xi[:, here], preferred_element_type=F32)
             weights = jnp.exp2(dist * (KERNEL_SCALE / F * math.log2(math.e)))
             aff[pl.ds(base, 2 * GROUP), here] = weights.astype(BF16)
+
+    def vector_tiles(q, src, rows):
+        base = pl.multiple_of(q * 2 * GROUP, 2 * GROUP)
+        groups = rows // 16
+        for half in range(2):
+            for b in range(4):
+                at = base + half * GROUP + b * LANES
+                panel[0:rows, pl.ds(at, LANES)] = src[half, q * 4 + b, 0:rows, :]
+            tile = tails_of([src[half, q * 4 + b, rows : rows + 16, :] for b in range(4)])[0:groups]
+            at = base + half * GROUP + 4 * LANES
+            panel[0:rows, pl.ds(at, LANES)] = jnp.concatenate(tile, axis=0).astype(BF16)
+
+    def product(q, rows):
+        base = pl.multiple_of(q * 2 * GROUP, 2 * GROUP)
         for c in range(ROWS_I // 256):
             here = slice(c * 256, (c + 1) * 256)
-            acc[0 : K + 16, here] += jnp.dot(
-                panel[0 : K + 16, pl.ds(base, 2 * GROUP)],
+            acc[0:rows, here] += jnp.dot(
+                panel[0:rows, pl.ds(base, 2 * GROUP)],
                 aff[pl.ds(base, 2 * GROUP), here],
                 preferred_element_type=F32,
             )
 
-    in_groups([(xy_copy, forward), (v_copy, v_forward)], first_work, "a")
-
-    blocks8 = lane_block()
+    with jax.named_scope("a_first_wait"):
+        arrived(0, v_copy, v_forward)
+
+    def work(q):
+        vector_tiles(q, vbuf, K)
+        affinity(q)
+        product(q, K + 16)
+
+    def step(q, carry):
+        with jax.named_scope("a_wait"):
+            arrived(q + 1, xy_copy, forward)
+            arrived(q + 1, v_copy, v_forward)
+            forwarded(q, forward)
+            forwarded(q, v_forward)
+        with jax.named_scope("a_work"):
+            work(q)
+        return carry
+
+    lax.fori_loop(0, 3, step, 0)
+    with jax.named_scope("a_last_wait"):
+        forwarded(3, forward)
+        forwarded(3, v_forward)
+    with jax.named_scope("a_last"):
+        work(3)
 
     def p_copy(it, d):
-        rows = K + 16 - 8 * it
-        return remote(
-            psend.at[it, d, pl.ds(0, rows)], precv.at[it, d, pl.ds(0, rows)],
-            p_s.at[it, d], p_r.at[it, d], z_peer(-d),
-        )
+        return remote(psend.at[it, d], precv.at[it, d], p_s.at[it, d], p_r.at[it, d], z_peer(-d))
+
+    blocks16 = lax.broadcasted_iota(jnp.int32, (16, LANES), 1) // TAIL
+    rows16 = lax.broadcasted_iota(jnp.int32, (16, LANES), 0)
 
     def send_product(it):
         for q in range(NZ // 4):
             at = NZ * LANES + q * LANES
-            tail = acc[0:K, at : at + LANES]
-            if it == 1:
-                tail = tail + acc[K : 2 * K, at : at + LANES]
-            packed = [
-                pick(blocks8, [roll_lanes(tail[8 * g : 8 * g + 8], TAIL * (g - b)) for g in range(4)])
-                for b in range(4)
-            ]
             for b in range(4):
                 d = 4 * q + b
-                main = acc[0:K, d * LANES : (d + 1) * LANES]
-                if it == 1:
-                    main = main + acc[K : 2 * K, d * LANES : (d + 1) * LANES]
-                psend[it, d, 0:K, :] = main
-                psend[it, d, K : K + 8, :] = packed[b]
+                here = slice(d * LANES, (d + 1) * LANES)
+                psend[it, d, 0:K, :] = acc[0:K, here].astype(BF16)
+                last = jnp.zeros((16, LANES), F32)
                 if it == 0:
-                    psend[it, d, K + 8 : K + 9, :] = acc[K : K + 1, d * LANES : (d + 1) * LANES]
-                    psend[it, d, K + 9 : K + 10, :] = roll_lanes(
-                        acc[K : K + 8, at : at + LANES], -TAIL * b
-                    )[0:1]
-                    psend[it, d, K + 10 : K + 16, :] = jnp.zeros((6, LANES), F32)
+                    hi, mid, _ = bf16_pieces(acc[K : K + 8, here])
+                    hi_t, mid_t, _ = bf16_pieces(acc[K : K + 8, at : at + LANES])
+                    lines = [
+                        roll_lanes(hi_t, TAIL * (2 - b)), roll_lanes(mid_t, TAIL * (2 - b)),
+                        roll_lanes(hi, 64), hi, roll_lanes(mid, 64), mid,
+                    ]
+                    for r, line in enumerate(lines):
+                        last = jnp.where(rows16 == r, line[0:1], last)
+                last = jnp.where(blocks16 == 0, roll_lanes(acc[0:16, at : at + LANES], -TAIL * b), last)
+                last = jnp.where(blocks16 == 1, roll_lanes(acc[16:32, at : at + LANES], TAIL * (1 - b)), last)
+                psend[it, d, K : K + 16, :] = last.astype(BF16)
         for d in (4, 3, 5, 2, 6, 1, 7):
             p_copy(it, d).start()
 
     def received_product(it):
-        rows = K + 16 - 8 * it
-        total = psend[it, 0, 0:rows]
+        total = psend[it, 0].astype(F32)
         for d in (1, 7, 2, 6, 3, 5, 4):
             p_copy(it, d).wait_recv()
-            total = total + precv[it, d, 0:rows]
+            total = total + precv[it, d].astype(F32)
         return total
+
+    def degree_of(total):
+        tail = roll_lanes(total[K : K + 1] + total[K + 1 : K + 2], 64)
+        low = roll_lanes(total[K + 2 : K + 3] + total[K + 4 : K + 5], 64)
+        high = total[K + 3 : K + 4] + total[K + 5 : K + 6]
+        lane = lax.broadcasted_iota(jnp.int32, (1, LANES), 1)
+        return jnp.where(lane < 64, low, high), jnp.where(lane < TAIL, tail, 1.0)
 
     def gram_of(scaled):
         wide = jnp.concatenate([scaled, jnp.zeros((LANES - K, 2 * LANES), F32)], axis=0)
@@ -389,40 +399,49 @@
     with jax.named_scope("reduce1"):
         total = received_product(0)
     with jax.named_scope("scale1"):
-        keep = lax.broadcasted_iota(jnp.int32, (1, LANES), 1) < TAIL
-        deg_main = total[K + 8 : K + 9]
-        deg_tail = jnp.where(keep, total[K + 9 : K + 10], 1.0)
+        deg_main, deg_tail = degree_of(total)
         scaled_main = total[0:K] / deg_main
-        scaled_tail = unpacked_tail(total[K : K + 8], 4) / deg_tail
+        scaled_tail = unpacked_tail(total[K : K + 16], 2) / deg_tail
         scaled = jnp.concatenate([scaled_main, scaled_tail], axis=1)
 
-        hi = scaled.astype(BF16).astype(F32)
-        lo = scaled - hi
-        both = jnp.concatenate([hi, lo], axis=0)
-        sbuf[0, 0, 0:64, :] = both[:, 0:LANES].astype(BF16)
-        sbuf[0, 0, 64:80, :] = packed_tail(both[:, LANES:], 16).astype(BF16)
+        both = scaled
+        if WIDE == 2:
+            hi = scaled.astype(BF16).astype(F32)
+            both = jnp.concatenate([hi, scaled - hi], axis=0)
+        sbuf[0, 0, 0 : WIDE * K, :] = both[:, 0:LANES].astype(BF16)
+        sbuf[0, 0, WIDE * K : WIDE * K + 16, :] = packed_tail(both[:, LANES:], 16).astype(BF16)
         for e in range(1, NXY):
             s_copy(e).start()
+        s_forward(0).start()
     with jax.named_scope("gram_first1"):
         gram_first(0, scaled)
         acc[...] = jnp.zeros_like(acc)
 
-    def second_work(q):
-        base = pl.multiple_of(q * 2 * GROUP, 2 * GROUP)
-        for half in range(2):
-            for b in range(4):
-                at = base + half * GROUP + b * LANES
-                panel[0 : 2 * K, pl.ds(at, LANES)] = sbuf[half, q * 4 + b, 0:64, :]
-            tile = tails_of([sbuf[half, q * 4 + b, 64:80, :] for b in range(4)])
-            at = base + half * GROUP + 4 * LANES
-            panel[0 : 2 * K, pl.ds(at, LANES)] = jnp.concatenate(tile, axis=0).astype(BF16)
-        acc[...] += jnp.dot(
-            panel[:, pl.ds(base, 2 * GROUP)],
-            aff[pl.ds(base, 2 * GROUP), :],
-            preferred_element_type=F32,
-        )
-
-    in_groups([(s_copy, s_forward)], second_work, "b", lambda: gram_second(0))
+    with jax.named_scope("b_first_wait"):
+        arrived(0, s_copy, s_forward)
+        arrived(1, s_copy, s_forward)
+        forwarded(0, s_forward)
+    with jax.named_scope("b_first"):
+        vector_tiles(0, sbuf, WIDE * K)
+        product(0, WIDE * K)
+    with jax.named_scope("b_second_wait"):
+        arrived(2, s_copy, s_forward)
+        forwarded(1, s_forward)
+    with jax.named_scope("b_second"):
+        vector_tiles(1, sbuf, WIDE * K)
+        product(1, WIDE * K)
+    with jax.named_scope("b_third_wait"):
+        arrived(3, s_copy, s_forward)
+        forwarded(2, s_forward)
+    with jax.named_scope("b_third"):
+        vector_tiles(2, sbuf, WIDE * K)
+        product(2, WIDE * K)
+    gram_second(0)
+    with jax.named_scope("b_last_wait"):
+        forwarded(3, s_forward)
+    with jax.named_scope("b_last"):
+        vector_tiles(3, sbuf, WIDE * K)
+        product(3, WIDE * K)
 
     eye = (
         lax.broadcasted_iota(jnp.int32, (K, LANES), 0)
@@ -438,7 +457,7 @@
         total = received_product(1)
     with jax.named_scope("scale2"):
         scaled = jnp.concatenate(
-            [total[0:K] / deg_main, unpacked_tail(total[K : K + 8], 4) / deg_tail], axis=1
+            [total[0:K] / deg_main, unpacked_tail(total[K : K + 16], 2) / deg_tail], axis=1
         )
         tall = jnp.concatenate([scaled, jnp.zeros((LANES - K, 2 * LANES), F32)], axis=0)
         scaled = jnp.dot(inverse, tall, precision=HIGHEST, preferred_element_type=F32)
@@ -490,9 +509,9 @@
                 pltpu.VMEM((2 * K, COLS_J), BF16),
                 pltpu.VMEM((COLS_J, ROWS_I), BF16),
                 pltpu.VMEM((2 * K, ROWS_I), F32),
-                pltpu.VMEM((2, NZ, K + 16, LANES), F32),
-                pltpu.VMEM((2, NZ, K + 16, LANES), F32),
-                pltpu.VMEM((2, NXY, 80, LANES), BF16),
+                pltpu.VMEM((2, NZ, K + 16, LANES), BF16),
+                pltpu.VMEM((2, NZ, K + 16, LANES), BF16),
+                pltpu.VMEM((2, NXY, WIDE * K + 16, LANES), BF16),
                 pltpu.VMEM((2, 2, 8, LANES), F32),
                 pltpu.VMEM((2, 2, 16, 8, LANES), F32),
                 dma((2,)),

time: 65 us -> 60.9 us (0.937)
  Pallas kernels: 62.7 us -> 58.6 us
    pallas_call x1, Pallas kernels: 62.7 us -> 58.6 us  [shards(): pl.pallas_call(kernel, out_shape=jax.ShapeDtypeStruct((K, OWN), F32), in_...]
where the time goes in v4:
time: 60.9 us; the launch traced here: 60.7 us
  Pallas kernels  58.6 us (96%)
  local copies, waits for them, and re-layouts  2.09 us (3%)
    pallas_call x1, Pallas kernels, shards(): pl.pallas_call(kernel, out_shape=jax.ShapeDtypeStruct((K, OWN), F32), in_...  58.6 us
    unnamed x5, local copies, waits for them, and re-layouts  2.09 us

profile of v4, /device:TPU:1, one launch (start us, length us, event | category | flops | bytes accessed | tf_op | source)
XLA Modules:
  0.0 60.7 jit_solution(10414964003108295847)
XLA Ops:
  0.0 0.0 copy-start
  0.0 0.8 %copy-done = bf16[160,64]{0,1:T(8,128)(2,1)S(1)} copy-done((bf16[160,64]{0,1:T(8,128)(2,1)S(1)}, bf16[160,64]{0,1:T(8,128)(2,1)}, u32[]{:S(2)}) %copy-start) | copy-done | bytes 20504
  0.8 0.0 copy-start.1
  0.8 0.7 %copy-done.1 = bf16[160,32]{0,1:T(8,128)(2,1)S(1)} copy-done((bf16[160,32]{0,1:T(8,128)(2,1)S(1)}, bf16[160,32]{0,1:T(8,128)(2,1)}, u32[]{:S(2)}) %copy-start.1) | copy-done | bytes 10264
  1.5 58.6 %shard_map.28 = f32[32,160]{1,0:T(8,128)S(1)} custom-call(bf16[64,160]{1,0:T(8,128)(2,1)S(1)} %bitcast.4, bf16[32,160]{1,0:T(8,128)(2,1)S(1)} %bitcast.5), custom_call_target="tpu_custom_call" | custom-call | tf_op jit(solution)/shard_map/pallas_call | solution.py:495
  60.1 0.6 %copy.4 = f32[160,32]{0,1:T(8,128)} copy(f32[160,32]{0,1:T(8,128)S(1)} %bitcast.3) | data formatting | bytes 40960
Async XLA Ops:
  0.0 0.8 %copy-start = (bf16[160,64]{0,1:T(8,128)(2,1)S(1)}, bf16[160,64]{0,1:T(8,128)(2,1)}, u32[]{:S(2)}) copy-start(bf16[160,64]{0,1:T(8,128)(2,1)} %param.2) | copy-start | bytes 61444
  0.8 0.7 %copy-start.1 = (bf16[160,32]{0,1:T(8,128)(2,1)S(1)}, bf16[160,32]{0,1:T(8,128)(2,1)}, u32[]{:S(2)}) copy-start(bf16[160,32]{0,1:T(8,128)(2,1)} %param.3) | copy-start | bytes 30724

commit v5 on v4

--- a/solution.py
+++ b/solution.py
@@ -129,9 +129,9 @@
 
 def kernel(
     pts_hbm, vec_hbm, out_ref,
-    pts_ref, vec_ref, stage, zbuf, jbuf, vbuf, xi, xj, panel, aff, acc, psend, precv, sbuf, gsend, grecv,
+    pts_ref, vec_ref, stage, zbuf, jbuf, vbuf, xi, xj, panel, aff, acc, kept, psend, precv, sbuf, gsend, grecv,
     in_s, z_s, z_r, xy_s, xy_r, f_s, f_r, v_s, v_r, vf_s, vf_r,
-    p_s, p_r, s_s, s_r, sf_s, sf_r, ga_s, ga_r, gb_s, gb_r,
+    p_s, p_r, s_s, s_r, sf_s, sf_r, g_s, g_r,
 ):
     row = lax.axis_index("row")
     col = lax.axis_index("col")
@@ -190,53 +190,52 @@
         pl.semaphore_wait(barrier, NCOL - 1 + NXY - 1)
 
     def z_copy(d):
-        return remote(jbuf.at[0, 0], zbuf.at[d], z_s.at[d], z_r.at[d], z_peer(d))
-
-    def xy_copy(e):
-        return remote(jbuf.at[0, 0], jbuf.at[0, e], xy_s.at[e], xy_r.at[e], xy_peer(e))
-
-    def forward(e):
-        return remote(jbuf.at[0, e], jbuf.at[1, e], f_s.at[e], f_r.at[e], partner)
-
-    def v_copy(e):
-        return remote(vbuf.at[0, 0], vbuf.at[0, e], v_s.at[e], v_r.at[e], xy_peer(e))
-
-    def v_forward(e):
-        return remote(vbuf.at[0, e], vbuf.at[1, e], vf_s.at[e], vf_r.at[e], partner)
-
-    def s_copy(e):
-        return remote(sbuf.at[0, 0], sbuf.at[0, e], s_s.at[e], s_r.at[e], xy_peer(e))
-
-    def s_forward(e):
-        return remote(sbuf.at[0, e], sbuf.at[1, e], sf_s.at[e], sf_r.at[e], partner)
-
-    def arrived(q, copy, onward):
-        for b in range(4):
-            e = q * 4 + b
-            if isinstance(e, int) and e == 0:
-                continue
-            copy(e).wait_recv()
-            onward(e).start()
-
-    def forwarded(q, onward):
-        for b in range(4):
-            onward(q * 4 + b).wait_recv()
+        return remote(jbuf.at[0, 0], zbuf.at[d], z_s, z_r.at[d], z_peer(d))
+
+    class Gathered:
+        def __init__(self, buf, send, recv, on_send, on_recv):
+            self.buf, self.send, self.recv, self.on_send, self.on_recv = buf, send, recv, on_send, on_recv
+
+        def start(self, e):
+            buf = self.buf
+            remote(buf.at[0, 0], buf.at[0, e], self.send, self.recv.at[e // 4], xy_peer(e)).start()
+
+        def group(self, q):
+            pieces = [self.buf.at[half, pl.ds(q * 4, 4)] for half in range(2)]
+            return remote(*pieces, self.on_send, self.on_recv.at[q], partner)
+
+        def arrived(self, q):
+            first, count = (1, 3) if isinstance(q, int) and q == 0 else (q * 4, 4)
+            piece = self.buf.at[0, pl.ds(first, count)]
+            remote(piece, piece, self.send, self.recv.at[q], partner).wait_recv()
+            self.group(q).start()
+
+        def forwarded(self, q):
+            self.group(q).wait_recv()
+
+        def sent(self):
+            piece = self.buf.at[0, pl.ds(1, NXY - 1)]
+            remote(piece, piece, self.send, self.recv.at[0], partner).wait_send()
+            piece = self.buf.at[0]
+            remote(piece, piece, self.on_send, self.on_recv.at[0], partner).wait_send()
+
+    points = Gathered(jbuf, xy_s, xy_r, f_s, f_r)
+    vectors = Gathered(vbuf, v_s, v_r, vf_s, vf_r)
+    scaleds = Gathered(sbuf, s_s, s_r, sf_s, sf_r)
 
     with jax.named_scope("send_points"):
         for d in (4, 3, 5, 2, 6, 1, 7):
             z_copy(d).start()
-        for e in range(1, NXY):
-            xy_copy(e).start()
-        forward(0).start()
-        for e in range(1, NXY):
-            v_copy(e).start()
-        v_forward(0).start()
+        for q in range(NXY // 4):
+            for gathered in (points, vectors):
+                for e in range(max(1, 4 * q), 4 * q + 4):
+                    gathered.start(e)
 
     def tails_of(tiles):
         return transposed_blocks([tile.astype(F32) for tile in tiles])
 
     with jax.named_scope("first_points"):
-        arrived(0, xy_copy, forward)
+        points.arrived(0)
 
     with jax.named_scope("row_side"):
         for d in range(NZ):
@@ -293,7 +292,7 @@
             )
 
     with jax.named_scope("a_first_wait"):
-        arrived(0, v_copy, v_forward)
+        vectors.arrived(0)
 
     def work(q):
         vector_tiles(q, vbuf, K)
@@ -302,23 +301,28 @@
 
     def step(q, carry):
         with jax.named_scope("a_wait"):
-            arrived(q + 1, xy_copy, forward)
-            arrived(q + 1, v_copy, v_forward)
-            forwarded(q, forward)
-            forwarded(q, v_forward)
+            points.arrived(q + 1)
+            vectors.arrived(q + 1)
+            points.forwarded(q)
+            vectors.forwarded(q)
         with jax.named_scope("a_work"):
             work(q)
         return carry
 
     lax.fori_loop(0, 3, step, 0)
     with jax.named_scope("a_last_wait"):
-        forwarded(3, forward)
-        forwarded(3, v_forward)
+        points.forwarded(3)
+        vectors.forwarded(3)
     with jax.named_scope("a_last"):
         work(3)
 
     def p_copy(it, d):
-        return remote(psend.at[it, d], precv.at[it, d], p_s.at[it, d], p_r.at[it, d], z_peer(-d))
+        return remote(psend.at[it, d], precv.at[it, d], p_s.at[it], p_r.at[it], z_peer(-d))
+
+    def p_all(it):
+        return remote(
+            psend.at[it, pl.ds(1, NZ - 1)], precv.at[it, pl.ds(1, NZ - 1)], p_s.at[it], p_r.at[it], partner
+        )
 
     blocks16 = lax.broadcasted_iota(jnp.int32, (16, LANES), 1) // TAIL
     rows16 = lax.broadcasted_iota(jnp.int32, (16, LANES), 0)
@@ -329,7 +333,8 @@
             for b in range(4):
                 d = 4 * q + b
                 here = slice(d * LANES, (d + 1) * LANES)
-                psend[it, d, 0:K, :] = acc[0:K, here].astype(BF16)
+                if d > 0:
+                    psend[it, d, 0:K, :] = acc[0:K, here].astype(BF16)
                 last = jnp.zeros((16, LANES), F32)
                 if it == 0:
                     hi, mid, _ = bf16_pieces(acc[K : K + 8, here])
@@ -342,14 +347,18 @@
                         last = jnp.where(rows16 == r, line[0:1], last)
                 last = jnp.where(blocks16 == 0, roll_lanes(acc[0:16, at : at + LANES], -TAIL * b), last)
                 last = jnp.where(blocks16 == 1, roll_lanes(acc[16:32, at : at + LANES], TAIL * (1 - b)), last)
-                psend[it, d, K : K + 16, :] = last.astype(BF16)
+                if d > 0:
+                    psend[it, d, K : K + 16, :] = last.astype(BF16)
+                else:
+                    kept[0:K, :] = acc[0:K, here]
+                    kept[K : K + 16, :] = last
         for d in (4, 3, 5, 2, 6, 1, 7):
             p_copy(it, d).start()
 
     def received_product(it):
-        total = psend[it, 0].astype(F32)
-        for d in (1, 7, 2, 6, 3, 5, 4):
-            p_copy(it, d).wait_recv()
+        p_all(it).wait_recv()
+        total = kept[...]
+        for d in range(1, NZ):
             total = total + precv[it, d].astype(F32)
         return total
 
@@ -367,32 +376,32 @@
         )
         return packed_tail(part, 8)
 
-    def ga_copy(it, d):
-        return remote(gsend.at[it, 0], grecv.at[it, 0, d], ga_s.at[it, d], ga_r.at[it, d], col_peer(d))
-
-    def gb_copy(it, e):
-        return remote(gsend.at[it, 1], grecv.at[it, 1, e], gb_s.at[it, e], gb_r.at[it, e], xy_peer(e))
+    def g_copy(it, stage, n, to):
+        return remote(gsend.at[it, stage], grecv.at[it, stage, n], g_s.at[it, stage], g_r.at[it, stage], to)
+
+    def g_all(it, stage):
+        piece = grecv.at[it, stage, pl.ds(1, 15)]
+        return remote(piece, piece, g_s.at[it, stage], g_r.at[it, stage], partner)
+
+    def g_total(it, stage):
+        g_all(it, stage).wait_recv()
+        terms = [gsend[it, stage]] + [grecv[it, stage, n] for n in range(1, 16)]
+        while len(terms) > 1:
+            terms = [a + b for a, b in zip(terms[::2], terms[1::2])]
+        return terms[0]
 
     def gram_first(it, scaled):
         gsend[it, 0] = gram_of(scaled)
-        for d in range(1, NCOL):
-            ga_copy(it, d).start()
+        for d in (8, 7, 9, 6, 10, 5, 11, 4, 12, 3, 13, 2, 14, 1, 15):
+            g_copy(it, 0, d, col_peer(d)).start()
 
     def gram_second(it):
-        total = gsend[it, 0]
-        for d in range(1, NCOL):
-            ga_copy(it, d).wait_recv()
-            total = total + grecv[it, 0, d]
-        gsend[it, 1] = total
-        for e in range(1, NXY):
-            gb_copy(it, e).start()
+        gsend[it, 1] = g_total(it, 0)
+        for e in range(NXY - 1, 0, -1):
+            g_copy(it, 1, e, xy_peer(e)).start()
 
     def gram_last(it):
-        total = gsend[it, 1]
-        for e in range(1, NXY):
-            gb_copy(it, e).wait_recv()
-            total = total + grecv[it, 1, e]
-        return unpacked_tail(total, 4) * (1.0 / TOTAL)
+        return unpacked_tail(g_total(it, 1), 4) * (1.0 / TOTAL)
 
     with jax.named_scope("send1"):
         send_product(0)
@@ -411,34 +420,33 @@
         sbuf[0, 0, 0 : WIDE * K, :] = both[:, 0:LANES].astype(BF16)
         sbuf[0, 0, WIDE * K : WIDE * K + 16, :] = packed_tail(both[:, LANES:], 16).astype(BF16)
         for e in range(1, NXY):
-            s_copy(e).start()
-        s_forward(0).start()
+            scaleds.start(e)
     with jax.named_scope("gram_first1"):
         gram_first(0, scaled)
         acc[...] = jnp.zeros_like(acc)
 
     with jax.named_scope("b_first_wait"):
-        arrived(0, s_copy, s_forward)
-        arrived(1, s_copy, s_forward)
-        forwarded(0, s_forward)
+        scaleds.arrived(0)
+        scaleds.arrived(1)
+        scaleds.forwarded(0)
     with jax.named_scope("b_first"):
         vector_tiles(0, sbuf, WIDE * K)
         product(0, WIDE * K)
     with jax.named_scope("b_second_wait"):
-        arrived(2, s_copy, s_forward)
-        forwarded(1, s_forward)
+        scaleds.arrived(2)
+        scaleds.forwarded(1)
     with jax.named_scope("b_second"):
         vector_tiles(1, sbuf, WIDE * K)
         product(1, WIDE * K)
     with jax.named_scope("b_third_wait"):
-        arrived(3, s_copy, s_forward)
-        forwarded(2, s_forward)
+        scaleds.arrived(3)
+        scaleds.forwarded(2)
     with jax.named_scope("b_third"):
         vector_tiles(2, sbuf, WIDE * K)
         product(2, WIDE * K)
     gram_second(0)
     with jax.named_scope("b_last_wait"):
-        forwarded(3, s_forward)
+        scaleds.forwarded(3)
     with jax.named_scope("b_last"):
         vector_tiles(3, sbuf, WIDE * K)
         product(3, WIDE * K)
@@ -463,29 +471,26 @@
         scaled = jnp.dot(inverse, tall, precision=HIGHEST, preferred_element_type=F32)
     with jax.named_scope("gram_first2"):
         gram_first(1, scaled)
+    with jax.named_scope("sent"):
+        piece = zbuf.at[pl.ds(1, NZ - 1)]
+        remote(piece, piece, z_s, z_r.at[0], partner).wait_send()
+        for gathered in (points, vectors, scaleds):
+            gathered.sent()
+        for it in range(2):
+            p_all(it).wait_send()
+        for stage in range(2):
+            g_all(0, stage).wait_send()
     with jax.named_scope("gram_second2"):
         gram_second(1)
     with jax.named_scope("gram_last2"):
+        g_all(1, 0).wait_send()
         last = gram_last(1)
     with jax.named_scope("eliminate2"):
         ortho = eliminate(last, scaled)
         out_ref[...] = ortho[:, 0:OWN]
 
-    for d in range(1, NZ):
-        z_copy(d).wait_send()
-        for it in range(2):
-            p_copy(it, d).wait_send()
-    for e in range(NXY):
-        forward(e).wait_send()
-        v_forward(e).wait_send()
-        s_forward(e).wait_send()
-    for e in range(1, NXY):
-        xy_copy(e).wait_send()
-        v_copy(e).wait_send()
-        s_copy(e).wait_send()
-        for it in range(2):
-            ga_copy(it, e).wait_send()
-            gb_copy(it, e).wait_send()
+    with jax.named_scope("drain"):
+        g_all(1, 1).wait_send()
 
 
 def solution(mesh):
@@ -509,27 +514,24 @@
                 pltpu.VMEM((2 * K, COLS_J), BF16),
                 pltpu.VMEM((COLS_J, ROWS_I), BF16),
                 pltpu.VMEM((2 * K, ROWS_I), F32),
+                pltpu.VMEM((K + 16, LANES), F32),
                 pltpu.VMEM((2, NZ, K + 16, LANES), BF16),
                 pltpu.VMEM((2, NZ, K + 16, LANES), BF16),
                 pltpu.VMEM((2, NXY, WIDE * K + 16, LANES), BF16),
                 pltpu.VMEM((2, 2, 8, LANES), F32),
                 pltpu.VMEM((2, 2, 16, 8, LANES), F32),
                 dma((2,)),
-                dma((NZ,)), dma((NZ,)),
-                dma((NXY,)), dma((NXY,)),
-                dma((NXY,)), dma((NXY,)),
-                dma((NXY,)), dma((NXY,)),
-                dma((NXY,)), dma((NXY,)),
-                dma((2, NZ)), dma((2, NZ)),
-                dma((NXY,)), dma((NXY,)),
-                dma((NXY,)), dma((NXY,)),
-                dma((2, NCOL)), dma((2, NCOL)),
-                dma((2, NXY)), dma((2, NXY)),
+                dma, dma((NZ,)),
+                dma, dma((4,)), dma, dma((4,)),
+                dma, dma((4,)), dma, dma((4,)),
+                dma((2,)), dma((2,)),
+                dma, dma((4,)), dma, dma((4,)),
+                dma((2, 2)), dma((2, 2)),
             ],
             compiler_params=pltpu.CompilerParams(
                 collective_id=0, has_side_effects=True, vmem_limit_bytes=48 * 1024 * 1024
             ),
-        )(points.T, start_vectors.T).T
+        )(*(pltpu.with_memory_space_constraint(v.T, pltpu.HBM) for v in (points, start_vectors))).T
 
     spec = P(("row", "col"), None)
     return jax.shard_map(

time: 60.9 us -> 55.5 us (0.911)
  Pallas kernels: 58.6 us -> 54.7 us
  local copies, waits for them, and re-layouts: 2.09 us -> 0.62 us
    pallas_call x1, Pallas kernels: 58.6 us -> 54.7 us  [shards(): pl.pallas_call(kernel, out_shape=jax.ShapeDtypeStruct((K, OWN), F32), in_...]
    unnamed x5 -> x1, local copies, waits for them, and re-layouts: 2.09 us -> 0.62 us
where the time goes in v5:
time: 55.5 us; the launch traced here: 55.3 us
  Pallas kernels  54.7 us (99%)
  local copies, waits for them, and re-layouts  0.62 us (1%)
    pallas_call x1, Pallas kernels, shards(): pl.pallas_call(kernel, out_shape=jax.ShapeDtypeStruct((K, OWN), F32), in_...  54.7 us

profile of v5, /device:TPU:1, one launch (start us, length us, event | category | flops | bytes accessed | tf_op | source)
XLA Modules:
  0.0 55.3 jit_solution(6606394832900274773)
XLA Ops:
  0.0 54.7 %shard_map.28 = f32[32,160]{1,0:T(8,128)S(1)} custom-call(bf16[64,160]{1,0:T(8,128)(2,1)} %bitcast.4, bf16[32,160]{1,0:T(8,128)(2,1)} %bitcast.5), custom_call_target="tpu_custom_call" | custom-call | tf_op jit(solution)/shard_map/pallas_call | solution.py:500
  54.7 0.6 %copy.4 = f32[160,32]{0,1:T(8,128)} copy(f32[160,32]{0,1:T(8,128)S(1)} %bitcast.3) | data formatting | bytes 40960

commit v6 on v5

--- a/solution.py
+++ b/solution.py
@@ -14,7 +14,6 @@
 HIGHEST = lax.Precision.HIGHEST
 
 KERNEL_SCALE = 5.12
-WIDE = 1
 F = 64
 K = 32
 OWN = 160
@@ -196,28 +195,34 @@
         def __init__(self, buf, send, recv, on_send, on_recv):
             self.buf, self.send, self.recv, self.on_send, self.on_recv = buf, send, recv, on_send, on_recv
 
-        def start(self, e):
-            buf = self.buf
-            remote(buf.at[0, 0], buf.at[0, e], self.send, self.recv.at[e // 4], xy_peer(e)).start()
-
-        def group(self, q):
-            pieces = [self.buf.at[half, pl.ds(q * 4, 4)] for half in range(2)]
-            return remote(*pieces, self.on_send, self.on_recv.at[q], partner)
-
-        def arrived(self, q):
-            first, count = (1, 3) if isinstance(q, int) and q == 0 else (q * 4, 4)
-            piece = self.buf.at[0, pl.ds(first, count)]
-            remote(piece, piece, self.send, self.recv.at[q], partner).wait_recv()
-            self.group(q).start()
-
-        def forwarded(self, q):
-            self.group(q).wait_recv()
+        def start(self, p):
+            for e in range(max(1, 8 * p), 8 * p + 8):
+                remote(
+                    self.buf.at[0, 0], self.buf.at[0, e], self.send.at[p], self.recv.at[p], xy_peer(e)
+                ).start()
+
+        def piece(self, p):
+            first = max(1, 8 * p)
+            piece = self.buf.at[0, pl.ds(first, 8 * p + 8 - first)]
+            return remote(piece, piece, self.send.at[p], self.recv.at[p], partner)
+
+        def group(self, p):
+            pieces = [self.buf.at[half, pl.ds(p * 8, 8)] for half in range(2)]
+            return remote(*pieces, self.on_send.at[p], self.on_recv.at[p], partner)
+
+        def arrived(self, p):
+            self.piece(p).wait_recv()
+            self.group(p).start()
+
+        def forwarded(self, p):
+            self.group(p).wait_recv()
+
+        def left(self, p):
+            self.piece(p).wait_send()
 
         def sent(self):
-            piece = self.buf.at[0, pl.ds(1, NXY - 1)]
-            remote(piece, piece, self.send, self.recv.at[0], partner).wait_send()
-            piece = self.buf.at[0]
-            remote(piece, piece, self.on_send, self.on_recv.at[0], partner).wait_send()
+            for p in range(2):
+                self.group(p).wait_send()
 
     points = Gathered(jbuf, xy_s, xy_r, f_s, f_r)
     vectors = Gathered(vbuf, v_s, v_r, vf_s, vf_r)
@@ -226,10 +231,13 @@
     with jax.named_scope("send_points"):
         for d in (4, 3, 5, 2, 6, 1, 7):
             z_copy(d).start()
-        for q in range(NXY // 4):
-            for gathered in (points, vectors):
-                for e in range(max(1, 4 * q), 4 * q + 4):
-                    gathered.start(e)
+        points.start(0)
+    with jax.named_scope("left_points"):
+        points.left(0)
+        vectors.start(0)
+        points.start(1)
+        vectors.left(0)
+        vectors.start(1)
 
     def tails_of(tiles):
         return transposed_blocks([tile.astype(F32) for tile in tiles])
@@ -254,15 +262,18 @@
             at = NZ * LANES + q * LANES
             xi[:, at : at + LANES] = extended(tile, True).astype(BF16)
 
-    def affinity(q):
-        base = pl.multiple_of(q * 2 * GROUP, 2 * GROUP)
-        for half in range(2):
-            for b in range(4):
-                at = half * GROUP + b * LANES
-                src = jbuf[half, q * 4 + b, 0:64, :].astype(F32)
+    def slots(h, sub):
+        return [(h % 2, h // 2 * 8 + sub * 4 + b) for b in range(4)]
+
+    def affinity(h):
+        base = pl.multiple_of(h * 2 * GROUP, 2 * GROUP)
+        for sub in range(2):
+            for b, (core_set, e) in enumerate(slots(h, sub)):
+                at = sub * GROUP + b * LANES
+                src = jbuf[core_set, e, 0:64, :].astype(F32)
                 xj[at : at + LANES, :] = extended(src, False).T.astype(BF16)
-            at = half * GROUP + 4 * LANES
-            tile = tails_of([jbuf[half, q * 4 + b, 64:80, :] for b in range(4)])
+            at = sub * GROUP + 4 * LANES
+            tile = tails_of([jbuf[core_set, e, 64:80, :] for core_set, e in slots(h, sub)])
             xj[at : at + LANES, :] = extended(jnp.concatenate(tile, axis=0), False).T.astype(BF16)
         for c in range(ROWS_I // 256):
             here = slice(c * 256, (c + 1) * 256)
@@ -270,19 +281,18 @@
             weights = jnp.exp2(dist * (KERNEL_SCALE / F * math.log2(math.e)))
             aff[pl.ds(base, 2 * GROUP), here] = weights.astype(BF16)
 
-    def vector_tiles(q, src, rows):
-        base = pl.multiple_of(q * 2 * GROUP, 2 * GROUP)
-        groups = rows // 16
-        for half in range(2):
-            for b in range(4):
-                at = base + half * GROUP + b * LANES
-                panel[0:rows, pl.ds(at, LANES)] = src[half, q * 4 + b, 0:rows, :]
-            tile = tails_of([src[half, q * 4 + b, rows : rows + 16, :] for b in range(4)])[0:groups]
-            at = base + half * GROUP + 4 * LANES
-            panel[0:rows, pl.ds(at, LANES)] = jnp.concatenate(tile, axis=0).astype(BF16)
-
-    def product(q, rows):
-        base = pl.multiple_of(q * 2 * GROUP, 2 * GROUP)
+    def vector_tiles(h, src):
+        base = pl.multiple_of(h * 2 * GROUP, 2 * GROUP)
+        for sub in range(2):
+            for b, (core_set, e) in enumerate(slots(h, sub)):
+                at = base + sub * GROUP + b * LANES
+                panel[0:K, pl.ds(at, LANES)] = src[core_set, e, 0:K, :]
+            tile = tails_of([src[core_set, e, K : K + 16, :] for core_set, e in slots(h, sub)])[0:2]
+            at = base + sub * GROUP + 4 * LANES
+            panel[0:K, pl.ds(at, LANES)] = jnp.concatenate(tile, axis=0).astype(BF16)
+
+    def product(h, rows):
+        base = pl.multiple_of(h * 2 * GROUP, 2 * GROUP)
         for c in range(ROWS_I // 256):
             here = slice(c * 256, (c + 1) * 256)
             acc[0:rows, here] += jnp.dot(
@@ -291,30 +301,31 @@
                 preferred_element_type=F32,
             )
 
+    def next_wait(h, gathered):
+        for step, waits in ((1, "forwarded"), (2, "arrived"), (3, "forwarded")):
+
+            @pl.when(h == step)
+            def _():
+                for g in gathered:
+                    getattr(g, waits)(step // 2)
+
+    def first_step(h, carry):
+        with jax.named_scope("a_wait"):
+            next_wait(h, (points, vectors))
+        with jax.named_scope("a_work"):
+            vector_tiles(h, vbuf)
+            affinity(h)
+            product(h, K + 16)
+        return carry
+
+    with jax.named_scope("a_first"):
+        affinity(0)
     with jax.named_scope("a_first_wait"):
         vectors.arrived(0)
-
-    def work(q):
-        vector_tiles(q, vbuf, K)
-        affinity(q)
-        product(q, K + 16)
-
-    def step(q, carry):
-        with jax.named_scope("a_wait"):
-            points.arrived(q + 1)
-            vectors.arrived(q + 1)
-            points.forwarded(q)
-            vectors.forwarded(q)
-        with jax.named_scope("a_work"):
-            work(q)
-        return carry
-
-    lax.fori_loop(0, 3, step, 0)
-    with jax.named_scope("a_last_wait"):
-        points.forwarded(3)
-        vectors.forwarded(3)
-    with jax.named_scope("a_last"):
-        work(3)
+    with jax.named_scope("a_first_product"):
+        vector_tiles(0, vbuf)
+        product(0, K + 16)
+    lax.fori_loop(1, 4, first_step, 0)
 
     def p_copy(it, d):
         return remote(psend.at[it, d], precv.at[it, d], p_s.at[it], p_r.at[it], z_peer(-d))
@@ -413,43 +424,36 @@
         scaled_tail = unpacked_tail(total[K : K + 16], 2) / deg_tail
         scaled = jnp.concatenate([scaled_main, scaled_tail], axis=1)
 
-        both = scaled
-        if WIDE == 2:
-            hi = scaled.astype(BF16).astype(F32)
-            both = jnp.concatenate([hi, scaled - hi], axis=0)
-        sbuf[0, 0, 0 : WIDE * K, :] = both[:, 0:LANES].astype(BF16)
-        sbuf[0, 0, WIDE * K : WIDE * K + 16, :] = packed_tail(both[:, LANES:], 16).astype(BF16)
-        for e in range(1, NXY):
-            scaleds.start(e)
+        sbuf[0, 0, 0:K, :] = scaled[:, 0:LANES].astype(BF16)
+        sbuf[0, 0, K : K + 16, :] = packed_tail(scaled[:, LANES:], 16).astype(BF16)
+        scaleds.start(0)
+        scaleds.start(1)
     with jax.named_scope("gram_first1"):
         gram_first(0, scaled)
-        acc[...] = jnp.zeros_like(acc)
-
-    with jax.named_scope("b_first_wait"):
+
+    with jax.named_scope("b_left"):
+        lo = (scaled - scaled.astype(BF16).astype(F32)).astype(BF16)
+        acc[0:K, :] = jnp.dot(lo[:, 0:LANES], aff[0:LANES, :], preferred_element_type=F32) + jnp.dot(
+            lo[:, LANES:], aff[4 * LANES : 5 * LANES, :], preferred_element_type=F32
+        )
+    with jax.named_scope("b_0_wait"):
         scaleds.arrived(0)
+    with jax.named_scope("b_0"):
+        vector_tiles(0, sbuf)
+        product(0, K)
+    with jax.named_scope("b_1_wait"):
         scaleds.arrived(1)
         scaleds.forwarded(0)
-    with jax.named_scope("b_first"):
-        vector_tiles(0, sbuf, WIDE * K)
-        product(0, WIDE * K)
-    with jax.named_scope("b_second_wait"):
-        scaleds.arrived(2)
+    with jax.named_scope("b_12"):
+        for h in (1, 2):
+            vector_tiles(h, sbuf)
+            product(h, K)
+    gram_second(0)
+    with jax.named_scope("b_3_wait"):
         scaleds.forwarded(1)
-    with jax.named_scope("b_second"):
-        vector_tiles(1, sbuf, WIDE * K)
-        product(1, WIDE * K)
-    with jax.named_scope("b_third_wait"):
-        scaleds.arrived(3)
-        scaleds.forwarded(2)
-    with jax.named_scope("b_third"):
-        vector_tiles(2, sbuf, WIDE * K)
-        product(2, WIDE * K)
-    gram_second(0)
-    with jax.named_scope("b_last_wait"):
-        scaleds.forwarded(3)
-    with jax.named_scope("b_last"):
-        vector_tiles(3, sbuf, WIDE * K)
-        product(3, WIDE * K)
+    with jax.named_scope("b_3"):
+        vector_tiles(3, sbuf)
+        product(3, K)
 
     eye = (
         lax.broadcasted_iota(jnp.int32, (K, LANES), 0)
@@ -474,6 +478,10 @@
     with jax.named_scope("sent"):
         piece = zbuf.at[pl.ds(1, NZ - 1)]
         remote(piece, piece, z_s, z_r.at[0], partner).wait_send()
+        points.left(1)
+        vectors.left(1)
+        for p in range(2):
+            scaleds.left(p)
         for gathered in (points, vectors, scaleds):
             gathered.sent()
         for it in range(2):
@@ -517,15 +525,15 @@
                 pltpu.VMEM((K + 16, LANES), F32),
                 pltpu.VMEM((2, NZ, K + 16, LANES), BF16),
                 pltpu.VMEM((2, NZ, K + 16, LANES), BF16),
-                pltpu.VMEM((2, NXY, WIDE * K + 16, LANES), BF16),
+                pltpu.VMEM((2, NXY, K + 16, LANES), BF16),
                 pltpu.VMEM((2, 2, 8, LANES), F32),
                 pltpu.VMEM((2, 2, 16, 8, LANES), F32),
                 dma((2,)),
                 dma, dma((NZ,)),
-                dma, dma((4,)), dma, dma((4,)),
-                dma, dma((4,)), dma, dma((4,)),
+                dma((2,)), dma((2,)), dma((2,)), dma((2,)),
+                dma((2,)), dma((2,)), dma((2,)), dma((2,)),
                 dma((2,)), dma((2,)),
-                dma, dma((4,)), dma, dma((4,)),
+                dma((2,)), dma((2,)), dma((2,)), dma((2,)),
                 dma((2, 2)), dma((2, 2)),
             ],
             compiler_params=pltpu.CompilerParams(

time: 55.5 us -> 54.1 us (0.975)
  Pallas kernels: 54.7 us -> 53.3 us
    pallas_call x1, Pallas kernels: 54.7 us -> 53.3 us  [shards(): pl.pallas_call(kernel, out_shape=jax.ShapeDtypeStruct((K, OWN), F32), in_...]
where the time goes in v6:
time: 54.1 us; the launch traced here: 53.9 us
  Pallas kernels  53.3 us (99%)
  local copies, waits for them, and re-layouts  0.62 us (1%)
    pallas_call x1, Pallas kernels, shards(): pl.pallas_call(kernel, out_shape=jax.ShapeDtypeStruct((K, OWN), F32), in_...  53.3 us

profile of v6, /device:TPU:1, one launch (start us, length us, event | category | flops | bytes accessed | tf_op | source)
XLA Modules:
  0.0 53.9 jit_solution(12214237924900422426)
XLA Ops:
  0.0 53.3 %shard_map.28 = f32[32,160]{1,0:T(8,128)S(1)} custom-call(bf16[64,160]{1,0:T(8,128)(2,1)} %bitcast.4, bf16[32,160]{1,0:T(8,128)(2,1)} %bitcast.5), custom_call_target="tpu_custom_call" | custom-call | tf_op jit(solution)/shard_map/pallas_call | solution.py:508
  53.3 0.6 %copy.4 = f32[160,32]{0,1:T(8,128)} copy(f32[160,32]{0,1:T(8,128)S(1)} %bitcast.3) | data formatting | bytes 40960

commit v7 on v6

--- a/solution.py
+++ b/solution.py
@@ -25,6 +25,7 @@
 NY = 4
 NXY = NX * NY
 NCOL = 2 * NZ
+FAR_FIRST = (8, 7, 9, 6, 10, 5, 11, 4, 12, 3, 13, 2, 14, 1, 15)
 ROWS_I = NZ * OWN
 COLS_J = 2 * NXY * OWN
 TOTAL = 256 * OWN
@@ -163,9 +164,9 @@
     vec_copy.start()
     barrier = pltpu.get_barrier_semaphore()
     with jax.named_scope("signal"):
-        for d in range(1, NCOL):
+        for d in FAR_FIRST:
             pl.semaphore_signal(barrier, inc=1, device_id=col_peer(d), device_id_type=MESH)
-        for e in range(1, NXY):
+        for e in range(NXY - 1, 0, -1):
             pl.semaphore_signal(barrier, inc=1, device_id=xy_peer(e), device_id_type=MESH)
 
     with jax.named_scope("prepare"):
@@ -246,7 +247,7 @@
         points.arrived(0)
 
     with jax.named_scope("row_side"):
-        for d in range(NZ):
+        for d in (0, 1, 7, 2, 6, 3, 5, 4):
             if d == 0:
                 src = jbuf[0, 0, 0:64, :]
             else:
@@ -271,10 +272,10 @@
             for b, (core_set, e) in enumerate(slots(h, sub)):
                 at = sub * GROUP + b * LANES
                 src = jbuf[core_set, e, 0:64, :].astype(F32)
-                xj[at : at + LANES, :] = extended(src, False).T.astype(BF16)
+                xj[at : at + LANES, :] = extended(src, False).astype(BF16).T
             at = sub * GROUP + 4 * LANES
             tile = tails_of([jbuf[core_set, e, 64:80, :] for core_set, e in slots(h, sub)])
-            xj[at : at + LANES, :] = extended(jnp.concatenate(tile, axis=0), False).T.astype(BF16)
+            xj[at : at + LANES, :] = extended(jnp.concatenate(tile, axis=0), False).astype(BF16).T
         for c in range(ROWS_I // 256):
             here = slice(c * 256, (c + 1) * 256)
             dist = jnp.dot(xj[...], xi[:, here], preferred_element_type=F32)
@@ -291,9 +292,9 @@
             at = base + sub * GROUP + 4 * LANES
             panel[0:K, pl.ds(at, LANES)] = jnp.concatenate(tile, axis=0).astype(BF16)
 
-    def product(h, rows):
+    def product(h, rows, chunks=range(ROWS_I // 256)):
         base = pl.multiple_of(h * 2 * GROUP, 2 * GROUP)
-        for c in range(ROWS_I // 256):
+        for c in chunks:
             here = slice(c * 256, (c + 1) * 256)
             acc[0:rows, here] += jnp.dot(
                 panel[0:rows, pl.ds(base, 2 * GROUP)],
@@ -301,32 +302,33 @@
                 preferred_element_type=F32,
             )
 
-    def next_wait(h, gathered):
-        for step, waits in ((1, "forwarded"), (2, "arrived"), (3, "forwarded")):
-
-            @pl.when(h == step)
-            def _():
-                for g in gathered:
-                    getattr(g, waits)(step // 2)
-
     def first_step(h, carry):
         with jax.named_scope("a_wait"):
-            next_wait(h, (points, vectors))
+
+            @pl.when(h == 1)
+            def _():
+                points.forwarded(0)
+                vectors.arrived(0)
+
+            @pl.when(h == 2)
+            def _():
+                points.arrived(1)
+                vectors.forwarded(0)
+
+            @pl.when(h == 3)
+            def _():
+                points.forwarded(1)
+                vectors.arrived(1)
+
         with jax.named_scope("a_work"):
-            vector_tiles(h, vbuf)
+            vector_tiles(h - 1, vbuf)
+            product(h - 1, K + 16)
             affinity(h)
-            product(h, K + 16)
         return carry
 
     with jax.named_scope("a_first"):
         affinity(0)
-    with jax.named_scope("a_first_wait"):
-        vectors.arrived(0)
-    with jax.named_scope("a_first_product"):
-        vector_tiles(0, vbuf)
-        product(0, K + 16)
     lax.fori_loop(1, 4, first_step, 0)
-
     def p_copy(it, d):
         return remote(psend.at[it, d], precv.at[it, d], p_s.at[it], p_r.at[it], z_peer(-d))
 
@@ -338,33 +340,34 @@
     blocks16 = lax.broadcasted_iota(jnp.int32, (16, LANES), 1) // TAIL
     rows16 = lax.broadcasted_iota(jnp.int32, (16, LANES), 0)
 
-    def send_product(it):
-        for q in range(NZ // 4):
-            at = NZ * LANES + q * LANES
-            for b in range(4):
-                d = 4 * q + b
-                here = slice(d * LANES, (d + 1) * LANES)
-                if d > 0:
-                    psend[it, d, 0:K, :] = acc[0:K, here].astype(BF16)
-                last = jnp.zeros((16, LANES), F32)
-                if it == 0:
-                    hi, mid, _ = bf16_pieces(acc[K : K + 8, here])
-                    hi_t, mid_t, _ = bf16_pieces(acc[K : K + 8, at : at + LANES])
-                    lines = [
-                        roll_lanes(hi_t, TAIL * (2 - b)), roll_lanes(mid_t, TAIL * (2 - b)),
-                        roll_lanes(hi, 64), hi, roll_lanes(mid, 64), mid,
-                    ]
-                    for r, line in enumerate(lines):
-                        last = jnp.where(rows16 == r, line[0:1], last)
-                last = jnp.where(blocks16 == 0, roll_lanes(acc[0:16, at : at + LANES], -TAIL * b), last)
-                last = jnp.where(blocks16 == 1, roll_lanes(acc[16:32, at : at + LANES], TAIL * (1 - b)), last)
-                if d > 0:
-                    psend[it, d, K : K + 16, :] = last.astype(BF16)
-                else:
-                    kept[0:K, :] = acc[0:K, here]
-                    kept[K : K + 16, :] = last
-        for d in (4, 3, 5, 2, 6, 1, 7):
+    def send_piece(it, d):
+        b, at = d % 4, NZ * LANES + d // 4 * LANES
+        here = slice(d * LANES, (d + 1) * LANES)
+        last = jnp.zeros((16, LANES), F32)
+        if it == 0:
+            hi, mid, _ = bf16_pieces(acc[K : K + 8, here])
+            hi_t, mid_t, _ = bf16_pieces(acc[K : K + 8, at : at + LANES])
+            lines = [
+                roll_lanes(hi_t, TAIL * (2 - b)), roll_lanes(mid_t, TAIL * (2 - b)),
+                roll_lanes(hi, 64), hi, roll_lanes(mid, 64), mid,
+            ]
+            for r, line in enumerate(lines):
+                last = jnp.where(rows16 == r, line[0:1], last)
+        last = jnp.where(blocks16 == 0, roll_lanes(acc[0:16, at : at + LANES], -TAIL * b), last)
+        last = jnp.where(blocks16 == 1, roll_lanes(acc[16:32, at : at + LANES], TAIL * (1 - b)), last)
+        if d == 0:
+            kept[0:K, :] = acc[0:K, here]
+            kept[K : K + 16, :] = last
+        else:
+            psend[it, d, 0:K, :] = acc[0:K, here].astype(BF16)
+            psend[it, d, K : K + 16, :] = last.astype(BF16)
             p_copy(it, d).start()
+
+    def last_product(it, rows):
+        for chunks, pieces in (((4, 2, 1), (4, 3, 5, 2)), ((3, 0), (6, 7, 1, 0))):
+            product(3, rows, chunks)
+            for d in pieces:
+                send_piece(it, d)
 
     def received_product(it):
         p_all(it).wait_recv()
@@ -403,7 +406,7 @@
 
     def gram_first(it, scaled):
         gsend[it, 0] = gram_of(scaled)
-        for d in (8, 7, 9, 6, 10, 5, 11, 4, 12, 3, 13, 2, 14, 1, 15):
+        for d in FAR_FIRST:
             g_copy(it, 0, d, col_peer(d)).start()
 
     def gram_second(it):
@@ -414,8 +417,11 @@
     def gram_last(it):
         return unpacked_tail(g_total(it, 1), 4) * (1.0 / TOTAL)
 
-    with jax.named_scope("send1"):
-        send_product(0)
+    with jax.named_scope("a_last_wait"):
+        vectors.forwarded(1)
+    with jax.named_scope("a_last"):
+        vector_tiles(3, vbuf)
+        last_product(0, K + 16)
     with jax.named_scope("reduce1"):
         total = received_product(0)
     with jax.named_scope("scale1"):
@@ -436,31 +442,27 @@
         acc[0:K, :] = jnp.dot(lo[:, 0:LANES], aff[0:LANES, :], preferred_element_type=F32) + jnp.dot(
             lo[:, LANES:], aff[4 * LANES : 5 * LANES, :], preferred_element_type=F32
         )
-    with jax.named_scope("b_0_wait"):
-        scaleds.arrived(0)
-    with jax.named_scope("b_0"):
-        vector_tiles(0, sbuf)
-        product(0, K)
-    with jax.named_scope("b_1_wait"):
-        scaleds.arrived(1)
-        scaleds.forwarded(0)
-    with jax.named_scope("b_12"):
-        for h in (1, 2):
+    def second_step(h):
+        with jax.named_scope("b_work"):
             vector_tiles(h, sbuf)
             product(h, K)
+
+    scaleds.arrived(0)
+    second_step(0)
+    scaleds.forwarded(0)
+    second_step(1)
+    scaleds.arrived(1)
+    second_step(2)
     gram_second(0)
-    with jax.named_scope("b_3_wait"):
-        scaleds.forwarded(1)
-    with jax.named_scope("b_3"):
+    scaleds.forwarded(1)
+    with jax.named_scope("b_last"):
         vector_tiles(3, sbuf)
-        product(3, K)
+        last_product(1, K)
 
     eye = (
         lax.broadcasted_iota(jnp.int32, (K, LANES), 0)
         == lax.broadcasted_iota(jnp.int32, (K, LANES), 1)
     ).astype(F32)
-    with jax.named_scope("send2"):
-        send_product(1)
     with jax.named_scope("gram_last1"):
         last = gram_last(0)
     with jax.named_scope("eliminate1"):

time: 54.1 us -> 52.7 us (0.974)
  Pallas kernels: 53.3 us -> 52 us
    pallas_call x1, Pallas kernels: 53.3 us -> 52 us  [shards(): pl.pallas_call(kernel, out_shape=jax.ShapeDtypeStruct((K, OWN), F32), in_...]
where the time goes in v7:
time: 52.7 us; the launch traced here: 52.6 us
  Pallas kernels  52 us (99%)
  local copies, waits for them, and re-layouts  0.62 us (1%)
    pallas_call x1, Pallas kernels, shards(): pl.pallas_call(kernel, out_shape=jax.ShapeDtypeStruct((K, OWN), F32), in_...  52 us

profile of v7, /device:TPU:1, one launch (start us, length us, event | category | flops | bytes accessed | tf_op | source)
XLA Modules:
  0.0 52.6 jit_solution(13712675105424528068)
XLA Ops:
  0.0 52.0 %shard_map.28 = f32[32,160]{1,0:T(8,128)S(1)} custom-call(bf16[64,160]{1,0:T(8,128)(2,1)} %bitcast.4, bf16[32,160]{1,0:T(8,128)(2,1)} %bitcast.5), custom_call_target="tpu_custom_call" | custom-call | tf_op jit(solution)/shard_map/pallas_call | solution.py:510
  52.0 0.6 %copy.4 = f32[160,32]{0,1:T(8,128)} copy(f32[160,32]{0,1:T(8,128)S(1)} %bitcast.3) | data formatting | bytes 40960

commit v8 on v7

--- a/solution.py
+++ b/solution.py
@@ -433,10 +433,10 @@
         sbuf[0, 0, 0:K, :] = scaled[:, 0:LANES].astype(BF16)
         sbuf[0, 0, K : K + 16, :] = packed_tail(scaled[:, LANES:], 16).astype(BF16)
         scaleds.start(0)
-        scaleds.start(1)
     with jax.named_scope("gram_first1"):
         gram_first(0, scaled)
 
+    scaleds.start(1)
     with jax.named_scope("b_left"):
         lo = (scaled - scaled.astype(BF16).astype(F32)).astype(BF16)
         acc[0:K, :] = jnp.dot(lo[:, 0:LANES], aff[0:LANES, :], preferred_element_type=F32) + jnp.dot(

time: 52.7 us -> 52.7 us (level)
  no operation moved by 1% of the time
where the time goes in v8:
time: 52.7 us; the launch traced here: 52.5 us
  Pallas kernels  51.9 us (98%)
  local copies, waits for them, and re-layouts  0.62 us (1%)
    pallas_call x1, Pallas kernels, shards(): pl.pallas_call(kernel, out_shape=jax.ShapeDtypeStruct((K, OWN), F32), in_...  51.9 us

profile of v8, /device:TPU:1, one launch (start us, length us, event | category | flops | bytes accessed | tf_op | source)
XLA Modules:
  0.0 52.5 jit_solution(1959836553424939387)
XLA Ops:
  0.0 51.9 %shard_map.28 = f32[32,160]{1,0:T(8,128)S(1)} custom-call(bf16[64,160]{1,0:T(8,128)(2,1)} %bitcast.4, bf16[32,160]{1,0:T(8,128)(2,1)} %bitcast.5), custom_call_target="tpu_custom_call" | custom-call | tf_op jit(solution)/shard_map/pallas_call | solution.py:510
  51.9 0.6 %copy.4 = f32[160,32]{0,1:T(8,128)} copy(f32[160,32]{0,1:T(8,128)S(1)} %bitcast.3) | data formatting | bytes 40960
